TPU v7x, 128 devices: a whole 4x4x4 slice. The times are simulated.
128 devices in a mesh: gx: 16 (over x, y), gy: 8 (over z, core).
Axes of the slice: x: 4, y: 4, z: 4, core: 2. Of those that a mesh axis runs over, the one named last changes fastest.
Arguments:
- cells: int32 [3, 4194304], P(None, ('gx', 'gy')), may hold values from 0 to 255, as said below
- fractions: float32 [3, 4194304], P(None, ('gx', 'gy')), may hold values from 0 to 1
- charges: float32 [4194304], P(('gx', 'gy')), may hold values from -24 to 24
- influence: float32 [256, 256, 256], P('gx', 'gy'), may hold values from 0.05 to 24, as said below
- shells: int32 [256, 256, 256], P('gx', 'gy'), may hold values from 0 to 255
Outputs:
- potential_hat: float32 [2, 256, 256, 256], P(None, 'gx', 'gy')
- energy: float32 [], replicated
- virial: float32 [3, 3], replicated
- spectrum: float32 [256], replicated
Inputs may be any that keep to these rules, and one draw needn't show every extreme that they name: `cells`: atom a belongs to device a // 32768, devices numbered with gy fastest; its y cell lies in that device's block of 16 y planes (block index its gx index) and its z cell in its block of 32 z planes (block index its gy index). `influence`: Positive.
All inputs are finite; a program needn't handle non-finite values.
Results may differ from a plain program's by a relative error of at most 0.0029.
Values sent between devices are 32-bit elements; how exact they have to be, the bound alone decides.
A program may use at most 64 MiB of HBM per device.

v0:
```python
import functools
import math

import jax
import jax.numpy as jnp
from jax import lax
from jax.sharding import Mesh
from jax.sharding import PartitionSpec as P

MESH = 256
SHELLS = 256
SCREEN = 4096
GX = ("gx_0", "gx_1")
GY = ("gy_0", "gy_1")
GX_GY = ("gx_0", "gx_1", "gy_0", "gy_1")


def passed_along(block, axis, distance):
    devices = range(lax.axis_size(axis))
    route = [((i - distance) % len(devices), i) for i in devices]
    return lax.ppermute(block, axis, route)


def cut_along(shard, dim, peers):
    lengths = shard.shape
    parts = shard.reshape(*lengths[:dim], peers, lengths[dim] // peers, *lengths[dim + 1 :])
    return jnp.moveaxis(parts, dim, 0)


def joined_along(parts, dim):
    lengths = list(parts.shape[1:])
    lengths[dim] *= parts.shape[0]
    return jnp.moveaxis(parts, 0, dim).reshape(lengths)


def moved_by_axis(parts, axes, turns):
    inside = parts.shape[1:]
    out = parts.reshape(*(lax.axis_size(a) for a in axes), *inside)
    for k in turns:
        out = lax.all_to_all(out, axes[k], k, k, tiled=True)
    return out.reshape(-1, *inside)


def one_axis_at_a_time(shard, axes, turns, split_dim, concat_dim):
    parts = cut_along(shard, split_dim, lax.axis_size(axes))
    return joined_along(moved_by_axis(parts, axes, turns), concat_dim)


def over_axes(shard, axes):
    return functools.reduce(lax.psum, axes, shard)


def spline(frac):
    cube = frac * frac * frac
    square = frac * frac
    rest = 1.0 - frac
    return (
        rest * rest * rest / 6.0,
        (3.0 * cube - 6.0 * square + 4.0) / 6.0,
        (-3.0 * cube + 3.0 * square + 3.0 * frac + 1.0) / 6.0,
        cube / 6.0,
    )


def place_weights(weights, target, columns, wrapped):
    result = jnp.zeros(columns.shape, jnp.float32)
    for offset in range(4):
        column = target[:, None] + offset
        if wrapped:
            column = column % MESH
        result = result + jnp.where(columns == column, weights[offset][:, None], 0.0)
    return result


def wave_tables():
    index = jnp.arange(MESH, dtype=jnp.int32)
    phase = index[:, None] * index[None, :] % MESH
    angle = phase.astype(jnp.float32) * (2.0 * math.pi / MESH)
    factor = 1.0 / math.sqrt(MESH)
    return (jnp.cos(angle) * factor, -jnp.sin(angle) * factor)


def wave_numbers(index):
    return jnp.where(index < MESH // 2, index, index - MESH).astype(jnp.float32)


def shards(cells, fractions, charges, influence, shells):
    rows_y = lax.axis_size(GX)
    cols_z = lax.axis_size(GY)
    plane_y = MESH // rows_y
    plane_z = MESH // cols_z
    first_y = lax.axis_index(GX) * plane_y
    first_z = lax.axis_index(GY) * plane_z
    ext_y = plane_y + 3
    ext_z = plane_z + 3
    count = charges.shape[0]
    block = min(2048, count)
    columns_x = lax.broadcasted_iota(jnp.int32, (block, MESH), 1)
    columns_y = lax.broadcasted_iota(jnp.int32, (block, ext_y), 1)
    columns_z = lax.broadcasted_iota(jnp.int32, (block, ext_z), 1)

    def spread(turn, accum):
        begin = turn * block
        cell = lax.dynamic_slice_in_dim(cells, begin, block, 1)
        frac = lax.dynamic_slice_in_dim(fractions, begin, block, 1)
        charge = lax.dynamic_slice_in_dim(charges, begin, block, 0)
        table_x = place_weights(spline(frac[0]), cell[0], columns_x, True)
        table_y = place_weights(spline(frac[1]), cell[1] - first_y, columns_y, False)
        wave_table_z = place_weights(spline(frac[2]), cell[2] - first_z, columns_z, False)
        factor_x = (charge[:, None] * table_x).astype(jnp.bfloat16)
        factor_yz = (
            (table_y[:, :, None] * wave_table_z[:, None, :])
            .reshape(block, ext_y * ext_z)
            .astype(jnp.bfloat16)
        )
        return accum + jnp.einsum(
            "ap,ax->px", factor_yz, factor_x, preferred_element_type=jnp.float32
        )

    spread_mesh = lax.fori_loop(
        0, count // block, spread, jnp.zeros((ext_y * ext_z, MESH), jnp.float32)
    )
    spread_mesh = spread_mesh.reshape(ext_y, ext_z, MESH)
    arrived = passed_along(spread_mesh[plane_y:], GX, 1)
    spread_mesh = spread_mesh[:plane_y].at[:3].add(arrived)
    arrived_z = passed_along(spread_mesh[:, plane_z:], GY, 1)
    spread_mesh = spread_mesh[:, :plane_z].at[:, :3].add(arrived_z)
    keep_y, keep_z = (plane_y, plane_z)
    cosine, minus_sine = wave_tables()
    real_table = jnp.stack([cosine, minus_sine])
    complex_table = jnp.stack([jnp.stack([cosine, -minus_sine]), jnp.stack([minus_sine, cosine])])
    upper_limit = lax.Precision.HIGHEST
    kx_rows = MESH // rows_y
    ky_rows = MESH // cols_z
    flat_mesh = spread_mesh.reshape(keep_y * keep_z, MESH)
    along_x = jnp.einsum("ckx,px->ckp", real_table, flat_mesh, precision=upper_limit)
    moved = lax.all_to_all(along_x[None], GX, split_axis=2, concat_axis=0, tiled=True)
    moved = moved.reshape(rows_y, 2, kx_rows, keep_y, keep_z)
    table_y = complex_table.reshape(2, 2, MESH, rows_y, plane_y)
    along_y = jnp.einsum("ocKst,scktz->okKz", table_y, moved, precision=upper_limit)
    shifted_along_z = one_axis_at_a_time(
        along_y.reshape(2, kx_rows, MESH * keep_z)[None], GY, (1, 0), 3, 0
    )
    shifted_along_z = shifted_along_z.reshape(cols_z, 2, kx_rows, ky_rows, keep_z)
    wave_table_z = complex_table.reshape(2, 2, MESH, cols_z, plane_z)
    structure_factor = jnp.einsum(
        "whzir,ihnqr->wnqz", wave_table_z, shifted_along_z, precision=upper_limit
    )
    wave_x = wave_numbers(lax.axis_index(GX) * kx_rows + jnp.arange(kx_rows, dtype=jnp.int32))[
        :, None, None
    ]
    wave_y = wave_numbers(lax.axis_index(GY) * ky_rows + jnp.arange(ky_rows, dtype=jnp.int32))[
        None, :, None
    ]
    wave_z = wave_numbers(jnp.arange(MESH, dtype=jnp.int32))[None, None, :]
    squared = wave_x * wave_x + wave_y * wave_y + wave_z * wave_z
    keep = jnp.where(squared > 0.0, 1.0, 0.0).astype(jnp.float32)
    weight = keep * influence
    potential_hat = structure_factor * weight[None]
    power = structure_factor[0] * structure_factor[0] + structure_factor[1] * structure_factor[1]
    influence_weighted = weight * power
    scale = 0.5 / MESH**3
    local_sum = jnp.sum(influence_weighted)
    coef = influence_weighted * 2.0 * (1.0 + squared / SCREEN) / (squared + 1.0 - keep)
    shape = coef.shape
    vectors = jnp.stack(
        [
            jnp.broadcast_to(wave_x, shape),
            jnp.broadcast_to(wave_y, shape),
            jnp.broadcast_to(wave_z, shape),
        ]
    )
    cross = jnp.einsum("akyz,bkyz->ab", vectors * coef[None], vectors, precision=upper_limit)
    virial_part = scale * (jnp.eye(3, dtype=jnp.float32) * local_sum - cross)
    energy_part = scale * local_sum
    shell_labels = jnp.arange(SHELLS, dtype=jnp.int32)

    def shell_rows(accum, pair):
        power_spectrum_row, shell_row = pair
        onehot = (shell_row.reshape(-1)[:, None] == shell_labels[None, :]).astype(jnp.float32)
        return (
            accum + jnp.dot(power_spectrum_row.reshape(-1), onehot, precision=upper_limit),
            None,
        )

    shell_sums, unused = lax.scan(shell_rows, jnp.zeros((SHELLS,), jnp.float32), (power, shells))
    spectrum_part = shell_sums * (SHELLS / MESH**3)
    energy, virial, spectrum = (
        over_axes(energy_part, GX_GY),
        over_axes(virial_part, GX_GY),
        over_axes(spectrum_part, GX_GY),
    )
    return (potential_hat, energy, virial, spectrum)


def solution(mesh):
    finer = Mesh(mesh.devices.reshape(4, 4, 4, 2), ("gx_0", "gx_1", "gy_0", "gy_1"))
    return jax.shard_map(
        shards,
        mesh=finer,
        in_specs=(P(None, GX_GY), P(None, GX_GY), P(GX_GY), P(GX, GY, None), P(GX, GY, None)),
        out_specs=(P(None, GX, GY, None), P(), P(), P()),
        check_vma=False,
    )
```

profile of v0, /device:TPU:1, one launch (start us, length us, event | category | flops | bytes accessed | tf_op | source)
XLA Modules:
  0.0 423.7 jit_solution(15081012513882294653)
XLA Ops:
  0.7 227.5 %while.31 = (s32[]{:T(128)}, f32[665,256]{1,0:T(8,128)}, s32[3,32768]{1,0:T(4,128)}, s32[]{:T(128)}, f32[3,32768]{1,0:T(4,128)}, /*index=5*/s32[]{:T(128)}, f32[...) while((s32[]{:T(128)}, f32[665,256]{1,0:T(8,128)}, ...), condition=%wide.region_1.2_spmd.clone.clone, body=%wide.region_0.1_spmd.clone.clone.sunk | while | flops 708628992 | bytes 13691121 | solution.py:120
  6.7 8.0 %convolution_add_fusion.2 = f32[665,256]{1,0:T(8,128)} fusion(bf16[2048,665]{0,1:T(8,128)(2,1)} %convert_element_type.169, f32[2048]{0:T(1024)S(1)} %get-tuple-element.612, s32[2048]{0:T(1024)S(1)} %get-tuple-element.614, f32[2048]{0:T(1024)S(1)} %get-tuple-element.615, s32[2048]{0:T(1024)S(1)} %get-tuple-element.616, ...), kind=kOutput, calls=%fused_computation.16.clone.1 | convolution fusion | flops 704459264 | bytes 4159489 | tf_op jit(solution)/shard_map/while/body/eval_jaxpr/ap,ax->px/dot_general | solution.py:116
  20.7 8.2 %convolution_add_fusion.2 = f32[665,256]{1,0:T(8,128)} fusion(bf16[2048,665]{0,1:T(8,128)(2,1)} %convert_element_type.169, f32[2048]{0:T(1024)S(1)} %get-tuple-element.612, s32[2048]{0:T(1024)S(1)} %get-tuple-element.614, f32[2048]{0:T(1024)S(1)} %get-tuple-element.615, s32[2048]{0:T(1024)S(1)} %get-tuple-element.616, ...), kind=kOutput, calls=%fused_computation.16.clone.1 | convolution fusion | flops 704459264 | bytes 4159489 | tf_op jit(solution)/shard_map/while/body/eval_jaxpr/ap,ax->px/dot_general | solution.py:116
  34.9 8.2 %convolution_add_fusion.2 = f32[665,256]{1,0:T(8,128)} fusion(bf16[2048,665]{0,1:T(8,128)(2,1)} %convert_element_type.169, f32[2048]{0:T(1024)S(1)} %get-tuple-element.612, s32[2048]{0:T(1024)S(1)} %get-tuple-element.614, f32[2048]{0:T(1024)S(1)} %get-tuple-element.615, s32[2048]{0:T(1024)S(1)} %get-tuple-element.616, ...), kind=kOutput, calls=%fused_computation.16.clone.1 | convolution fusion | flops 704459264 | bytes 4159489 | tf_op jit(solution)/shard_map/while/body/eval_jaxpr/ap,ax->px/dot_general | solution.py:116
  49.1 8.2 %convolution_add_fusion.2 = f32[665,256]{1,0:T(8,128)} fusion(bf16[2048,665]{0,1:T(8,128)(2,1)} %convert_element_type.169, f32[2048]{0:T(1024)S(1)} %get-tuple-element.612, s32[2048]{0:T(1024)S(1)} %get-tuple-element.614, f32[2048]{0:T(1024)S(1)} %get-tuple-element.615, s32[2048]{0:T(1024)S(1)} %get-tuple-element.616, ...), kind=kOutput, calls=%fused_computation.16.clone.1 | convolution fusion | flops 704459264 | bytes 4159489 | tf_op jit(solution)/shard_map/while/body/eval_jaxpr/ap,ax->px/dot_general | solution.py:116
  63.4 8.2 %convolution_add_fusion.2 = f32[665,256]{1,0:T(8,128)} fusion(bf16[2048,665]{0,1:T(8,128)(2,1)} %convert_element_type.169, f32[2048]{0:T(1024)S(1)} %get-tuple-element.612, s32[2048]{0:T(1024)S(1)} %get-tuple-element.614, f32[2048]{0:T(1024)S(1)} %get-tuple-element.615, s32[2048]{0:T(1024)S(1)} %get-tuple-element.616, ...), kind=kOutput, calls=%fused_computation.16.clone.1 | convolution fusion | flops 704459264 | bytes 4159489 | tf_op jit(solution)/shard_map/while/body/eval_jaxpr/ap,ax->px/dot_general | solution.py:116
  77.6 8.2 %convolution_add_fusion.2 = f32[665,256]{1,0:T(8,128)} fusion(bf16[2048,665]{0,1:T(8,128)(2,1)} %convert_element_type.169, f32[2048]{0:T(1024)S(1)} %get-tuple-element.612, s32[2048]{0:T(1024)S(1)} %get-tuple-element.614, f32[2048]{0:T(1024)S(1)} %get-tuple-element.615, s32[2048]{0:T(1024)S(1)} %get-tuple-element.616, ...), kind=kOutput, calls=%fused_computation.16.clone.1 | convolution fusion | flops 704459264 | bytes 4159489 | tf_op jit(solution)/shard_map/while/body/eval_jaxpr/ap,ax->px/dot_general | solution.py:116
  91.8 8.2 %convolution_add_fusion.2 = f32[665,256]{1,0:T(8,128)} fusion(bf16[2048,665]{0,1:T(8,128)(2,1)} %convert_element_type.169, f32[2048]{0:T(1024)S(1)} %get-tuple-element.612, s32[2048]{0:T(1024)S(1)} %get-tuple-element.614, f32[2048]{0:T(1024)S(1)} %get-tuple-element.615, s32[2048]{0:T(1024)S(1)} %get-tuple-element.616, ...), kind=kOutput, calls=%fused_computation.16.clone.1 | convolution fusion | flops 704459264 | bytes 4159489 | tf_op jit(solution)/shard_map/while/body/eval_jaxpr/ap,ax->px/dot_general | solution.py:116
  106.1 8.2 %convolution_add_fusion.2 = f32[665,256]{1,0:T(8,128)} fusion(bf16[2048,665]{0,1:T(8,128)(2,1)} %convert_element_type.169, f32[2048]{0:T(1024)S(1)} %get-tuple-element.612, s32[2048]{0:T(1024)S(1)} %get-tuple-element.614, f32[2048]{0:T(1024)S(1)} %get-tuple-element.615, s32[2048]{0:T(1024)S(1)} %get-tuple-element.616, ...), kind=kOutput, calls=%fused_computation.16.clone.1 | convolution fusion | flops 704459264 | bytes 4159489 | tf_op jit(solution)/shard_map/while/body/eval_jaxpr/ap,ax->px/dot_general | solution.py:116
  120.3 8.2 %convolution_add_fusion.2 = f32[665,256]{1,0:T(8,128)} fusion(bf16[2048,665]{0,1:T(8,128)(2,1)} %convert_element_type.169, f32[2048]{0:T(1024)S(1)} %get-tuple-element.612, s32[2048]{0:T(1024)S(1)} %get-tuple-element.614, f32[2048]{0:T(1024)S(1)} %get-tuple-element.615, s32[2048]{0:T(1024)S(1)} %get-tuple-element.616, ...), kind=kOutput, calls=%fused_computation.16.clone.1 | convolution fusion | flops 704459264 | bytes 4159489 | tf_op jit(solution)/shard_map/while/body/eval_jaxpr/ap,ax->px/dot_general | solution.py:116
  134.5 8.2 %convolution_add_fusion.2 = f32[665,256]{1,0:T(8,128)} fusion(bf16[2048,665]{0,1:T(8,128)(2,1)} %convert_element_type.169, f32[2048]{0:T(1024)S(1)} %get-tuple-element.612, s32[2048]{0:T(1024)S(1)} %get-tuple-element.614, f32[2048]{0:T(1024)S(1)} %get-tuple-element.615, s32[2048]{0:T(1024)S(1)} %get-tuple-element.616, ...), kind=kOutput, calls=%fused_computation.16.clone.1 | convolution fusion | flops 704459264 | bytes 4159489 | tf_op jit(solution)/shard_map/while/body/eval_jaxpr/ap,ax->px/dot_general | solution.py:116
  148.8 8.2 %convolution_add_fusion.2 = f32[665,256]{1,0:T(8,128)} fusion(bf16[2048,665]{0,1:T(8,128)(2,1)} %convert_element_type.169, f32[2048]{0:T(1024)S(1)} %get-tuple-element.612, s32[2048]{0:T(1024)S(1)} %get-tuple-element.614, f32[2048]{0:T(1024)S(1)} %get-tuple-element.615, s32[2048]{0:T(1024)S(1)} %get-tuple-element.616, ...), kind=kOutput, calls=%fused_computation.16.clone.1 | convolution fusion | flops 704459264 | bytes 4159489 | tf_op jit(solution)/shard_map/while/body/eval_jaxpr/ap,ax->px/dot_general | solution.py:116
  163.0 8.2 %convolution_add_fusion.2 = f32[665,256]{1,0:T(8,128)} fusion(bf16[2048,665]{0,1:T(8,128)(2,1)} %convert_element_type.169, f32[2048]{0:T(1024)S(1)} %get-tuple-element.612, s32[2048]{0:T(1024)S(1)} %get-tuple-element.614, f32[2048]{0:T(1024)S(1)} %get-tuple-element.615, s32[2048]{0:T(1024)S(1)} %get-tuple-element.616, ...), kind=kOutput, calls=%fused_computation.16.clone.1 | convolution fusion | flops 704459264 | bytes 4159489 | tf_op jit(solution)/shard_map/while/body/eval_jaxpr/ap,ax->px/dot_general | solution.py:116
  177.2 8.2 %convolution_add_fusion.2 = f32[665,256]{1,0:T(8,128)} fusion(bf16[2048,665]{0,1:T(8,128)(2,1)} %convert_element_type.169, f32[2048]{0:T(1024)S(1)} %get-tuple-element.612, s32[2048]{0:T(1024)S(1)} %get-tuple-element.614, f32[2048]{0:T(1024)S(1)} %get-tuple-element.615, s32[2048]{0:T(1024)S(1)} %get-tuple-element.616, ...), kind=kOutput, calls=%fused_computation.16.clone.1 | convolution fusion | flops 704459264 | bytes 4159489 | tf_op jit(solution)/shard_map/while/body/eval_jaxpr/ap,ax->px/dot_general | solution.py:116
  191.5 8.2 %convolution_add_fusion.2 = f32[665,256]{1,0:T(8,128)} fusion(bf16[2048,665]{0,1:T(8,128)(2,1)} %convert_element_type.169, f32[2048]{0:T(1024)S(1)} %get-tuple-element.612, s32[2048]{0:T(1024)S(1)} %get-tuple-element.614, f32[2048]{0:T(1024)S(1)} %get-tuple-element.615, s32[2048]{0:T(1024)S(1)} %get-tuple-element.616, ...), kind=kOutput, calls=%fused_computation.16.clone.1 | convolution fusion | flops 704459264 | bytes 4159489 | tf_op jit(solution)/shard_map/while/body/eval_jaxpr/ap,ax->px/dot_general | solution.py:116
  205.7 8.2 %convolution_add_fusion.2 = f32[665,256]{1,0:T(8,128)} fusion(bf16[2048,665]{0,1:T(8,128)(2,1)} %convert_element_type.169, f32[2048]{0:T(1024)S(1)} %get-tuple-element.612, s32[2048]{0:T(1024)S(1)} %get-tuple-element.614, f32[2048]{0:T(1024)S(1)} %get-tuple-element.615, s32[2048]{0:T(1024)S(1)} %get-tuple-element.616, ...), kind=kOutput, calls=%fused_computation.16.clone.1 | convolution fusion | flops 704459264 | bytes 4159489 | tf_op jit(solution)/shard_map/while/body/eval_jaxpr/ap,ax->px/dot_general | solution.py:116
  219.9 8.2 %convolution_add_fusion.2 = f32[665,256]{1,0:T(8,128)} fusion(bf16[2048,665]{0,1:T(8,128)(2,1)} %convert_element_type.169, f32[2048]{0:T(1024)S(1)} %get-tuple-element.612, s32[2048]{0:T(1024)S(1)} %get-tuple-element.614, f32[2048]{0:T(1024)S(1)} %get-tuple-element.615, s32[2048]{0:T(1024)S(1)} %get-tuple-element.616, ...), kind=kOutput, calls=%fused_computation.16.clone.1 | convolution fusion | flops 704459264 | bytes 4159489 | tf_op jit(solution)/shard_map/while/body/eval_jaxpr/ap,ax->px/dot_general | solution.py:116
  232.5 5.4 %collective-permute-done = f32[3,35,256]{2,1,0:T(8,128)S(1)} collective-permute-done((f32[3,35,256]{2,1,0:T(8,128)S(1)}, f32[3,35,256]{2,1,0:T(8,128)S(1)}, u32[]{:S(2)}, u32[]{:S(2)}) %collective-permute-start) | collective-permute-done | bytes 107552 | tf_op jit(solution)/shard_map/ppermute | solution.py:21
  245.2 3.8 all-to-all-start
  250.3 13.6 %all-to-all-done = f32[1,2,256,512]{3,1,0,2:T(2,128)S(1)} async-done(((f32[1,2,256,512]{3,1,0,2:T(2,128)}), f32[1,2,256,512]{3,1,0,2:T(2,128)S(1)}, u32[]{:S(2)}, u32[]{:S(2)}) %all-to-all-start) | async-done | bytes 1048608 | tf_op jit(solution)/shard_map/all_to_all | solution.py:137
  267.1 9.1 %fusion.63 = f32[2,16,256,32]{2,3,0,1:T(8,128)S(1)} fusion(f32[16,2,16,16,32,1]{4,3,0,1,2,5:T(8,128)} %reshape.1076, f32[1,1,256,16,16]{2,4,3,1,0:T(8,128)S(1)} %get-tuple-element.491, f32[1,1,256,16,16]{2,4,3,1,0:T(8,128)S(1)} %get-tuple-element.490, f32[1,1,256,16,16]{2,4,3,1,0:T(8,128)S(1)} %get-tuple-element.489), kind=kOutput, calls=%fused_computation.114 | convolution fusion | flops 1611399168 | bytes 2883584 | tf_op jit(solution)/shard_map/ocKst,scktz->okKz/dot_general | solution.py:140
  278.8 3.7 reshape_broadcast_in_dim_reshape.3
  283.6 7.2 %all_to_all.25 = f32[4,2,1,2,16,1024]{5,0,3,4,2,1:T(4,128)S(1)} all-to-all(f32[4,2,1,2,16,1024]{5,0,3,4,2,1:T(4,128)S(1)} %copy.18), channel_id=1, replica_groups=mesh['gx_0'=4,'gx_1'=4,'gy_0'=4,'gy_1'=2] {'gy_1'}, dimensions={1} | all-to-all | bytes 2097152 | tf_op jit(solution)/shard_map/all_to_all | solution.py:40
  292.6 5.1 %all-to-all-start.2 = ((f32[4,2,1,2,16,1024]{5,1,3,4,2,0:T(2,128)}), f32[4,2,1,2,16,1024]{5,1,3,4,2,0:T(2,128)S(1)}, u32[]{:S(2)}, u32[]{:S(2)}) async-start(f32[4,2,1,2,16,1024]{5,1,3,4,2,0:T(2,128)} %copy.19), calls=%async_computation.2 | async-start | bytes 2097152 | tf_op jit(solution)/shard_map/all_to_all | solution.py:40
  298.9 13.3 %all-to-all-done.2 = f32[4,2,1,2,16,1024]{5,1,3,4,2,0:T(2,128)S(1)} async-done(((f32[4,2,1,2,16,1024]{5,1,3,4,2,0:T(2,128)}), f32[4,2,1,2,16,1024]{5,1,3,4,2,0:T(2,128)S(1)}, u32[]{:S(2)}, u32[]{:S(2)}) %all-to-all-start.2) | async-done | bytes 1048608 | tf_op jit(solution)/shard_map/all_to_all | solution.py:40
  315.5 5.7 %fusion.66 = f32[2,16,32,256]{3,2,0,1:T(8,128)S(1)} fusion(f32[8,2,16,32,32,1]{4,3,0,1,2,5:T(8,128)} %reshape.1079, f32[1,1,256,8,32]{2,4,3,1,0:T(8,128)S(1)} %get-tuple-element.494, f32[1,1,256,8,32]{2,4,3,1,0:T(8,128)S(1)} %get-tuple-element.493, f32[1,1,256,8,32]{2,4,3,1,0:T(8,128)S(1)} %get-tuple-element.492), kind=kOutput, calls=%fused_computation.115 | convolution fusion | flops 1611399168 | bytes 2883584 | tf_op jit(solution)/shard_map/whzir,ihnqr->wnqz/dot_general | solution.py:146
  322.4 56.6 %while.30 = (s32[]{:T(128)}, f32[256]{0:T(256)S(1)}, f32[16,32,256]{2,1,0:T(8,128)S(1)}, s32[16,32,256]{2,1,0:T(8,128)}, s32[]{:T(128)}, /*index=5*/s32[]{:T(128)}) while((s32[]{:T(128)}, f32[256]{0:T(256)S(1)}, f32[16,32,256]{2,1,0:T(8,128)S(1)}, s32[16,32,256]{2,1,0:T(8,128)}, s32[]{:T(128)}, /*index=5*/s32[]{:T(128)}) %tuple.122), condition=%wide.region_12.13_spmd.clone, body=%wide.region_11.12_spmd.clone.sunk | while | flops 27263488 | bytes 331863 | solution.py:186
  380.8 10.1 %fusion.79 = f32[3,3]{1,0:T(4,128)S(1)} fusion(f32[1,16,32,256]{3,0,2,1:T(1,128)S(1)} %stack_broadcast_in_dim.8, f32[1,16,32,256]{3,0,2,1:T(1,128)S(1)} %stack_broadcast_in_dim.7, f32[1,16,32,256]{3,0,2,1:T(1,128)S(1)} %stack_broadcast_in_dim.6, f32[16,32,256]{2,1,0:T(8,128)S(1)} %get-tuple-element.456, f32[]{:T(128)} %multiply_reduce_fusion), kind=kOutput, calls=%fused_computation.119 | convolution fusion | flops 16121892 | bytes 2097192 | tf_op jit(solution)/shard_map/akyz,bkyz->ab/dot_general | solution.py:173
  391.9 6.8 %all-reduce.2 = (f32[]{:T(128)}, f32[3,3]{1,0:T(4,128)S(1)}, f32[256]{0:T(256)S(1)}) all-reduce(f32[]{:T(128)S(6)} %mul.997, f32[3,3]{1,0:T(4,128)S(1)} %fusion.79, f32[256]{0:T(256)S(1)} %broadcast_multiply_fusion.1), channel_id=1, replica_groups=mesh['gx_0'=4,'gx_1'=4,'gy_0'=4,'gy_1'=2] {'gx_0'}, use_global_device_ids=true, to_apply=%region_3.4 | all-reduce | flops 266 | bytes 2128 | tf_op jit(solution)/shard_map/psum | solution.py:50
  398.8 7.4 %all-reduce.1 = (f32[]{:T(128)}, f32[3,3]{1,0:T(4,128)S(1)}, f32[256]{0:T(256)S(1)}) all-reduce(f32[]{:T(128)} %get-tuple-element.450, f32[3,3]{1,0:T(4,128)S(1)} %get-tuple-element.451, f32[256]{0:T(256)S(1)} %get-tuple-element.452), channel_id=1, replica_groups=mesh['gx_0'=4,'gx_1'=4,'gy_0'=4,'gy_1'=2] {'gx_1'}, use_global_device_ids=true, to_apply=%region_4.5 | all-reduce | flops 266 | bytes 2128 | tf_op jit(solution)/shard_map/psum | solution.py:50
  406.1 7.5 %all-reduce = (f32[]{:T(128)}, f32[3,3]{1,0:T(4,128)S(1)}, f32[256]{0:T(256)S(1)}) all-reduce(f32[]{:T(128)} %get-tuple-element.447, f32[3,3]{1,0:T(4,128)S(1)} %get-tuple-element.448, f32[256]{0:T(256)S(1)} %get-tuple-element.449), channel_id=1, replica_groups=mesh['gx_0'=4,'gx_1'=4,'gy_0'=4,'gy_1'=2] {'gy_0'}, use_global_device_ids=true, to_apply=%region_5.6 | all-reduce | flops 266 | bytes 2128 | tf_op jit(solution)/shard_map/psum | solution.py:50
  413.6 10.1 %all-reduce.3 = (f32[]{:T(128)}, f32[3,3]{1,0:T(4,128)}, f32[256]{0:T(256)}) all-reduce(f32[]{:T(128)} %get-tuple-element.444, f32[3,3]{1,0:T(4,128)S(1)} %get-tuple-element.445, f32[256]{0:T(256)S(1)} %get-tuple-element.446), channel_id=1, replica_groups=mesh['gx_0'=4,'gx_1'=4,'gy_0'=4,'gy_1'=2] {'gy_1'}, use_global_device_ids=true, to_apply=%region_6.7 | all-reduce | flops 266 | bytes 2128 | tf_op jit(solution)/shard_map/psum | solution.py:50
  (351 shorter events, 180.1 us)
Async XLA Ops:
  229.1 8.8 %collective-permute-start = (f32[3,35,256]{2,1,0:T(8,128)S(1)}, f32[3,35,256]{2,1,0:T(8,128)S(1)}, u32[]{:S(2)}, u32[]{:S(2)}) collective-permute-start(f32[3,35,256]{2,1,0:T(8,128)S(1)} %slice.141), channel_id=1, source_target_pairs={{120,0},{0,8},{8,16},{16,24},{24,32},{32,40},{40,48},{48,56},{56,6... | collective-permute-start | bytes 322568 | tf_op jit(solution)/shard_map/ppermute | solution.py:21
  238.0 4.1 collective-permute-start.1
  245.2 18.7 %all-to-all-start = ((f32[1,2,256,512]{3,1,0,2:T(2,128)}), f32[1,2,256,512]{3,1,0,2:T(2,128)S(1)}, u32[]{:S(2)}, u32[]{:S(2)}) async-start(f32[1,2,256,512]{3,1,0,2:T(2,128)} %copy.15), calls=%async_computation | async-start | bytes 2097152 | tf_op jit(solution)/shard_map/all_to_all | solution.py:137
  292.6 19.6 %all-to-all-start.2 = ((f32[4,2,1,2,16,1024]{5,1,3,4,2,0:T(2,128)}), f32[4,2,1,2,16,1024]{5,1,3,4,2,0:T(2,128)S(1)}, u32[]{:S(2)}, u32[]{:S(2)}) async-start(f32[4,2,1,2,16,1024]{5,1,3,4,2,0:T(2,128)} %copy.19), calls=%async_computation.2 | async-start | bytes 2097152 | tf_op jit(solution)/shard_map/all_to_all | solution.py:40
  315.5 5.7 %copy-start = (f32[16,32,256]{2,1,0:T(8,128)S(1)}, f32[16,32,256]{2,1,0:T(8,128)}, u32[]{:S(2)}) copy-start(f32[16,32,256]{2,1,0:T(8,128)} %param.16) | copy-start | bytes 1572868
where the time goes:
time: 430 us; the launch traced here: 424 us
  matrix products  199 us (46%)
  local copies, waits for them, and re-layouts  100 us (23%)
  blocking collectives  39 us (9%)
  other arithmetic  35.2 us (8%)
  waiting for transfers between devices  32.6 us (8%)
  starting transfers between devices  13.9 us (3%)
    dot_general x16, matrix products, spread(): jnp.einsum('ap,ax->px', factor_yz, factor_x, preferred_element_type=jnp.f...  131 us
    dot_general x16, matrix products, shell_rows(): jnp.dot(power_spectrum_row.reshape(-1), onehot, precision=upper_limit)  42.2 us
    convert_element_type x16, local copies, waits for them, and re-layouts, spread(): factor_yz = (table_y[:, :, None] * wave_table_z[:, None, :]).reshape(bloc...  37.9 us
    psum x4, blocking collectives, over_axes(): return functools.reduce(lax.psum, axes, shard)  31.8 us
    slice x16, local copies, waits for them, and re-layouts, spread(): table_x = place_weights(spline(frac[0]), cell[0], columns_x, True)  15.5 us
    slice x16, other arithmetic, spread(): table_x = place_weights(spline(frac[0]), cell[0], columns_x, True)  15.5 us
    all_to_all x1, waiting for transfers between devices, shards(): lax.all_to_all(along_x[None], GX, split_axis=2, concat_axis=0, tiled=True)  13.6 us
    all_to_all x1, waiting for transfers between devices, moved_by_axis(): out = lax.all_to_all(out, axes[k], k, k, tiled=True)  13.3 us
  transfers between devices with their start and end apart: 4, of which 4 were waited for; matrix products, arithmetic and copies ran while one was open for 1% of the time, Pallas kernels for 0%

commit v1 on v0

v1 whole, which is shorter than its diff:
```python
import functools
import math

import jax
import jax.numpy as jnp
from jax import lax
from jax.experimental import pallas as pl
from jax.experimental.pallas import tpu as pltpu
from jax.sharding import Mesh
from jax.sharding import PartitionSpec as P

MESH = 256
SHELLS = 256
SCREEN = 4096
ROWS = 688
CHUNK = 1024
GX = ("gx_0", "gx_1")
GY = ("gy_0", "gy_1")
GX_GY = ("gx_0", "gx_1", "gy_0", "gy_1")


def passed_along(block, axis, distance):
    devices = range(lax.axis_size(axis))
    route = [((i - distance) % len(devices), i) for i in devices]
    return lax.ppermute(block, axis, route)


def cut_along(shard, dim, peers):
    lengths = shard.shape
    parts = shard.reshape(*lengths[:dim], peers, lengths[dim] // peers, *lengths[dim + 1 :])
    return jnp.moveaxis(parts, dim, 0)


def joined_along(parts, dim):
    lengths = list(parts.shape[1:])
    lengths[dim] *= parts.shape[0]
    return jnp.moveaxis(parts, 0, dim).reshape(lengths)


def moved_by_axis(parts, axes, turns):
    inside = parts.shape[1:]
    out = parts.reshape(*(lax.axis_size(a) for a in axes), *inside)
    for k in turns:
        out = lax.all_to_all(out, axes[k], k, k, tiled=True)
    return out.reshape(-1, *inside)


def one_axis_at_a_time(shard, axes, turns, split_dim, concat_dim):
    parts = cut_along(shard, split_dim, lax.axis_size(axes))
    return joined_along(moved_by_axis(parts, axes, turns), concat_dim)


def wave_tables():
    index = jnp.arange(MESH, dtype=jnp.int32)
    phase = index[:, None] * index[None, :] % MESH
    angle = phase.astype(jnp.float32) * (2.0 * math.pi / MESH)
    factor = 1.0 / math.sqrt(MESH)
    return (jnp.cos(angle) * factor, -jnp.sin(angle) * factor)


def spline(frac):
    cube = frac * frac * frac
    square = frac * frac
    rest = 1.0 - frac
    return (
        rest * rest * rest / 6.0,
        (3.0 * cube - 6.0 * square + 4.0) / 6.0,
        (-3.0 * cube + 3.0 * square + 3.0 * frac + 1.0) / 6.0,
        cube / 6.0,
    )


def periodic(cell, weights, rows, dim):
    row = lax.broadcasted_iota(jnp.int32, (rows, 128), 0)
    low = jnp.broadcast_to(cell[dim : dim + 1] & (rows - 1), (rows, 128))
    high = jnp.broadcast_to(cell[dim : dim + 1] // rows, (rows, 128))
    step = (row - low) & (rows - 1)
    table = jnp.zeros((rows, 128), jnp.float32)
    for t in range(4):
        table = jnp.where(step == t, jnp.broadcast_to(weights[t], (rows, 128)), table)
    block = high + jnp.where(row < low, 1, 0)
    return table, block


def build(cells_ref, frac_ref, charge_ref, begin, yz_buf, x_buf, XR=8):
    for tile in range(CHUNK // 128):
        at = pl.ds(pl.multiple_of(begin + tile * 128, 128), 128)
        lanes = pl.ds(tile * 128, 128)
        cell = cells_ref[:, at]
        weights = spline(frac_ref[:, at])
        charge = charge_ref[:, at]
        table, block = periodic(cell, [charge * w[0:1] for w in weights], 8, 0)
        block = block & 31
        for group in range(16):
            pair = [jnp.where(block == 2 * group + h, table, 0.0) for h in range(2)]
            x_buf[pl.ds(16 * group, 16), lanes] = jnp.concatenate(pair, 0).astype(jnp.bfloat16)
        table, block = periodic(cell & 15, [w[1:2] for w in weights], 8, 1)
        wy = [jnp.where(block == h, table, 0.0) for h in range(3)]
        table, block = periodic(cell & 31, [w[2:3] for w in weights], 8, 2)
        wz = [jnp.where(block == h, table, 0.0) for h in range(5)]
        for y in range(19):
            one = jnp.broadcast_to(wy[y // 8][y % 8 : y % 8 + 1], (8, 128))
            for half in range(2):
                pair = jnp.concatenate([one * wz[2 * half], one * wz[2 * half + 1]], 0)
                yz_buf[pl.ds(32 * y + 16 * half, 16), lanes] = pair.astype(jnp.bfloat16)
        tail = []
        for z in range(3):
            one = jnp.broadcast_to(wz[4][z : z + 1], (8, 128))
            tail += [one * wy[h] for h in range(3)]
        tail.append(jnp.zeros((8, 128), jnp.float32))
        for k in range(5):
            pair = jnp.concatenate(tail[2 * k : 2 * k + 2], 0)
            yz_buf[pl.ds(608 + 16 * k, 16), lanes] = pair.astype(jnp.bfloat16)


def product(yz_buf, x_buf):
    return lax.dot_general(
        yz_buf[...], x_buf[...], (((1,), (1,)), ((), ())), preferred_element_type=jnp.float32
    )


def spread_kernel(cells_ref, frac_ref, charge_ref, out_ref, yz0, x0, yz1, x1):
    count = charge_ref.shape[1]
    trips = count // (2 * CHUNK)
    out_ref[...] = jnp.zeros_like(out_ref)
    build(cells_ref, frac_ref, charge_ref, 0, yz0, x0)

    def body(m, carry):
        build(cells_ref, frac_ref, charge_ref, (2 * m + 1) * CHUNK, yz1, x1)
        out_ref[...] += product(yz0, x0)
        nxt = jnp.minimum((2 * m + 2) * CHUNK, count - CHUNK)
        build(cells_ref, frac_ref, charge_ref, nxt, yz0, x0)
        out_ref[...] += product(yz1, x1)
        return carry

    lax.fori_loop(0, trips, body, 0)


def spread(cells, fractions, charges):
    count = charges.shape[0]
    return pl.pallas_call(
        spread_kernel,
        out_shape=jax.ShapeDtypeStruct((ROWS, MESH), jnp.float32),
        in_specs=[pl.BlockSpec(memory_space=pltpu.VMEM)] * 3,
        out_specs=pl.BlockSpec(memory_space=pltpu.VMEM),
        scratch_shapes=[
            pltpu.VMEM((ROWS, CHUNK), jnp.bfloat16),
            pltpu.VMEM((MESH, CHUNK), jnp.bfloat16),
        ] * 2,
        compiler_params=pltpu.CompilerParams(vmem_limit_bytes=48 << 20),
        name="spread",
    )(cells, fractions, charges.reshape(1, count))


def signed(index):
    return jnp.where(index < MESH // 2, index, index - MESH).astype(jnp.float32)

def slab_outputs(real, imag, influence, shells, wave_x, wave_y, wave_z):
    squared = wave_x * wave_x + (wave_y * wave_y + wave_z * wave_z)
    origin = squared > 0.0
    weight = jnp.where(origin, influence, 0.0)
    power = real * real + imag * imag
    value = weight * power
    coef = value * 2.0 * (1.0 + squared * (1.0 / SCREEN)) / jnp.where(origin, squared, 1.0)
    return weight * real, weight * imag, power, value, coef

def onehot_dot(power, shells):
    total = None
    for r in range(4):
        p = power[8 * r : 8 * r + 8]
        s = shells[8 * r : 8 * r + 8]
        high = s >> 4
        low = s & 15
        left = jnp.concatenate([jnp.where(high == b, p, 0.0) for b in range(16)], 0).astype(jnp.bfloat16)
        right = jnp.concatenate([jnp.where(low == b, 1.0, 0.0) for b in range(16)], 0).astype(jnp.bfloat16)
        part = lax.dot_general(left, right, (((1,), (1,)), ((), ())), preferred_element_type=jnp.float32)
        total = part if total is None else total + part
    return total

def epilogue_kernel(s_ref, influence_ref, shells_ref, first_ref, pot_ref, stats_ref, hist, m0, m1, m2, en):
    first_x = first_ref[0]
    first_y = first_ref[1]
    rows = s_ref.shape[2]
    wave_y = signed(first_y + lax.broadcasted_iota(jnp.int32, (rows, MESH), 0))
    wave_z = signed(lax.broadcasted_iota(jnp.int32, (rows, MESH), 1))
    for ref in (hist, m0, m1, m2, en):
        ref[...] = jnp.zeros_like(ref)

    def body(k, carry):
        wave_x = signed(first_x + k)
        pr, pi, power, value, coef = slab_outputs(s_ref[0, k], s_ref[1, k], influence_ref[k], shells_ref[k], wave_x, wave_y, wave_z)
        pot_ref[0, k] = pr
        pot_ref[1, k] = pi
        hist[...] += onehot_dot(power, shells_ref[k])
        en[...] += value
        m0[...] += coef
        m1[...] += coef * wave_x
        m2[...] += coef * (wave_x * wave_x)
        return carry
    lax.fori_loop(0, s_ref.shape[1], body, 0)
    stats_ref[...] = pack_stats(hist[...], en[...], m0[...], m1[...], m2[...], wave_y, wave_z)

def thirds(x):
    a = x.astype(jnp.bfloat16)
    rest = x - a.astype(jnp.float32)
    b = rest.astype(jnp.bfloat16)
    c = (rest - b.astype(jnp.float32)).astype(jnp.bfloat16)
    return a, b, c

def pack_stats(hist, en, m0, m1, m2, wave_y, wave_z):
    row = lax.broadcasted_iota(jnp.int32, (128, 128), 0)
    col = lax.broadcasted_iota(jnp.int32, (128, 128), 1)
    diag = jnp.where((row & 7) == (col & 7), hist, 0.0)
    by_high = jnp.sum(diag.reshape(16, 8, 128), axis=1)
    pick = (lax.broadcasted_iota(jnp.int32, (128, 256), 0) >> 3) == (lax.broadcasted_iota(jnp.int32, (128, 256), 1) & 15)
    pick = jnp.where(pick, 1.0, 0.0).astype(jnp.bfloat16)
    wide = sum(jnp.dot(t, pick, preferred_element_type=jnp.float32) for t in thirds(by_high))
    own = lax.broadcasted_iota(jnp.int32, (16, 256), 0) == (lax.broadcasted_iota(jnp.int32, (16, 256), 1) >> 4)
    spectrum = jnp.sum(jnp.where(own, wide, 0.0), axis=0, keepdims=True)
    terms = [en, m2, m1 * wave_y, m1 * wave_z, m0 * wave_y * wave_y, m0 * wave_y * wave_z, m0 * wave_z * wave_z]
    sub = lax.broadcasted_iota(jnp.int32, (8, 256), 0)
    out = jnp.where(sub == 0, jnp.broadcast_to(spectrum, (8, 256)), 0.0)
    for n, t in enumerate(terms):
        line = jnp.sum(t.reshape(4, 8, 256), axis=0)
        line = jnp.sum(line, axis=0, keepdims=True)
        out = jnp.where(sub == n + 1, jnp.broadcast_to(line, (8, 256)), out)
    return out

def epilogue(structure, influence, shells, first):
    v = pl.BlockSpec(memory_space=pltpu.VMEM)
    rows = influence.shape[1]
    return pl.pallas_call(
        epilogue_kernel,
        out_shape=(jax.ShapeDtypeStruct(structure.shape, jnp.float32), jax.ShapeDtypeStruct((8, 256), jnp.float32)),
        in_specs=[v, v, v, pl.BlockSpec(memory_space=pltpu.SMEM)],
        out_specs=(v, v),
        scratch_shapes=[pltpu.VMEM((128, 128), jnp.float32)] + [pltpu.VMEM((rows, MESH), jnp.float32)] * 4,
        compiler_params=pltpu.CompilerParams(vmem_limit_bytes=48 << 20),
        name="epilogue",
    )(structure, influence, shells, first)


def shards(cells, fractions, charges, influence, shells):
    rows_y = lax.axis_size(GX)
    cols_z = lax.axis_size(GY)
    plane_y = MESH // rows_y
    plane_z = MESH // cols_z
    extended = spread(cells, fractions, charges)
    main = extended[: 19 * 32].reshape(19, 32, MESH)
    tail = extended[19 * 32 : 19 * 32 + 72].reshape(3, 24, MESH)[:, :19].transpose(1, 0, 2)
    spread_mesh = jnp.concatenate([main, tail], 1)
    arrived = passed_along(spread_mesh[plane_y:], GX, 1)
    spread_mesh = spread_mesh[:plane_y].at[:3].add(arrived)
    arrived_z = passed_along(spread_mesh[:, plane_z:], GY, 1)
    spread_mesh = spread_mesh[:, :plane_z].at[:, :3].add(arrived_z)
    keep_y, keep_z = (plane_y, plane_z)
    cosine, minus_sine = wave_tables()
    real_table = jnp.stack([cosine, minus_sine])
    complex_table = jnp.stack([jnp.stack([cosine, -minus_sine]), jnp.stack([minus_sine, cosine])])
    upper_limit = lax.Precision.HIGHEST
    kx_rows = MESH // rows_y
    ky_rows = MESH // cols_z
    flat_mesh = spread_mesh.reshape(keep_y * keep_z, MESH)
    along_x = jnp.einsum("ckx,px->ckp", real_table, flat_mesh, precision=upper_limit)
    moved = lax.all_to_all(along_x[None], GX, split_axis=2, concat_axis=0, tiled=True)
    moved = moved.reshape(rows_y, 2, kx_rows, keep_y, keep_z)
    table_y = complex_table.reshape(2, 2, MESH, rows_y, plane_y)
    along_y = jnp.einsum("ocKst,scktz->okKz", table_y, moved, precision=upper_limit)
    shifted_along_z = one_axis_at_a_time(
        along_y.reshape(2, kx_rows, MESH * keep_z)[None], GY, (1, 0), 3, 0
    )
    shifted_along_z = shifted_along_z.reshape(cols_z, 2, kx_rows, ky_rows, keep_z)
    wave_table_z = complex_table.reshape(2, 2, MESH, cols_z, plane_z)
    structure_factor = jnp.einsum(
        "whzir,ihnqr->wnqz", wave_table_z, shifted_along_z, precision=upper_limit
    )
    first = jnp.stack([lax.axis_index(GX) * kx_rows, lax.axis_index(GY) * ky_rows])
    potential_hat, stats = epilogue(structure_factor, influence, shells, first)
    stats = lax.psum(stats, GX_GY)
    scale = 0.5 / MESH**3
    spectrum = stats[0] * (SHELLS / MESH**3)
    sums = jnp.sum(stats[1:], axis=1)
    cross = jnp.stack([sums[1], sums[2], sums[3], sums[2], sums[4], sums[5], sums[3], sums[5], sums[6]])
    virial = scale * (jnp.eye(3, dtype=jnp.float32) * sums[0] - cross.reshape(3, 3))
    return (potential_hat, scale * sums[0], virial, spectrum)


def solution(mesh):
    finer = Mesh(mesh.devices.reshape(4, 4, 4, 2), ("gx_0", "gx_1", "gy_0", "gy_1"))
    return jax.shard_map(
        shards,
        mesh=finer,
        in_specs=(P(None, GX_GY), P(None, GX_GY), P(GX_GY), P(GX, GY, None), P(GX, GY, None)),
        out_specs=(P(None, GX, GY, None), P(), P(), P()),
        check_vma=False,
    )
```

time: 430 us -> 196 us (0.46); the launches traced: 424 us -> 196 us
  matrix products: 199 us -> 15.9 us
  local copies, waits for them, and re-layouts: 100 us -> 23 us
  blocking collectives: 39 us -> 70.4 us
  Pallas kernels: 0 us -> 30.9 us
  other arithmetic: 35.2 us -> 5.39 us
    dot_general x33 -> x0, matrix products: 183 us -> none  [the longest x16 131 us: spread(): jnp.einsum('ap,ax->px', factor_yz, factor_x, preferred_element_type=jnp.f...]
    convert_element_type x16 -> x0, local copies, waits for them, and re-layouts: 37.9 us -> none  [spread(): factor_yz = (table_y[:, :, None] * wave_table_z[:, None, :]).reshape(bloc...]
    psum x4 -> x1, blocking collectives: 31.8 us -> 63.2 us  [shards(): stats = lax.psum(stats, GX_GY)]
    pallas_call x0 -> x2, Pallas kernels: none -> 30.9 us  [the longest x1 25.6 us: spread(): pl.pallas_call(spread_kernel, out_shape=jax.ShapeDtypeStruct((ROWS, MESH)...]
    slice x20 -> x5, local copies, waits for them, and re-layouts: 17.7 us -> 0.85 us  [the longest x1 0.65 us: shards(): sums[3]]
    slice x16 -> x0, other arithmetic: 15.5 us -> none  [spread(): table_x = place_weights(spline(frac[0]), cell[0], columns_x, True)]
    while x64 -> x0, local copies, waits for them, and re-layouts: 13.3 us -> none
    dynamic_slice x16 -> x0, local copies, waits for them, and re-layouts: 11.3 us -> none  [spread(): charge = lax.dynamic_slice_in_dim(charges, begin, block, 0)]
  transfers between devices with their start and end apart: 4 -> 4, of which waited for: 4 -> 4; matrix products, arithmetic and copies ran while one was open for 1% -> 2% of each run, Pallas kernels for 0% -> 0%
where the time goes in v1:
time: 196 us
  blocking collectives  70.4 us (36%)
  waiting for transfers between devices  33.8 us (17%)
  Pallas kernels  30.9 us (16%)
  local copies, waits for them, and re-layouts  23 us (12%)
  matrix products  15.9 us (8%)
  starting transfers between devices  13.9 us (7%)
  other arithmetic  5.39 us (3%)
  between operations  2.59 us (1%)
    psum x1, blocking collectives, shards(): stats = lax.psum(stats, GX_GY)  63.2 us
    pallas_call x1, Pallas kernels, spread(): pl.pallas_call(spread_kernel, out_shape=jax.ShapeDtypeStruct((ROWS, MESH)...  25.6 us
    all_to_all x1, waiting for transfers between devices, shards(): lax.all_to_all(along_x[None], GX, split_axis=2, concat_axis=0, tiled=True)  13.7 us
    all_to_all x1, waiting for transfers between devices, moved_by_axis(): out = lax.all_to_all(out, axes[k], k, k, tiled=True)  13.3 us
    dot_general x1, matrix products, shards(): jnp.einsum('ocKst,scktz->okKz', table_y, moved, precision=upper_limit)  9.08 us
    all_to_all x1, blocking collectives, moved_by_axis(): out = lax.all_to_all(out, axes[k], k, k, tiled=True)  7.21 us
    ppermute x2, waiting for transfers between devices, passed_along(): return lax.ppermute(block, axis, route)  6.79 us
    dot_general x1, matrix products, shards(): jnp.einsum('whzir,ihnqr->wnqz', wave_table_z, shifted_along_z, precision=...  5.77 us
  transfers between devices with their start and end apart: 4, of which 4 were waited for; matrix products, arithmetic and copies ran while one was open for 2% of the time, Pallas kernels for 0%

profile of v1, /device:TPU:1, one launch (start us, length us, event | category | flops | bytes accessed | tf_op | source)
XLA Modules:
  0.0 195.9 jit_solution(6650360977851933123)
XLA Ops:
  0.6 1.0 copy-done
  1.7 1.0 copy-done.1
  2.7 0.9 copy-done.4
  3.6 25.6 %spread.1 = f32[688,256]{1,0:T(8,128)S(1)} custom-call(s32[3,32768]{1,0:T(4,128)S(1)} %copy-done, f32[3,32768]{1,0:T(4,128)S(1)} %copy-done.1, f32[1,32768]{1,0:T(1,128)S(1)} %bitcast.58), custom_call_target="tpu_custom_call" | custom-call | tf_op jit(solution)/shard_map/spread/pallas_call | solution.py:141
  29.4 2.2 %collective-permute-start = (f32[3,35,256]{2,1,0:T(8,128)S(1)}, f32[3,35,256]{2,1,0:T(8,128)S(1)}, u32[]{:S(2)}, u32[]{:S(2)}) collective-permute-start(f32[3,35,256]{2,1,0:T(8,128)S(1)} %pad_maximum_fusion), channel_id=1, source_target_pairs={{120,0},{0,8},{8,16},{16,24},{24,32},{32,40},{40,48},{48,56},{56,6... | collective-permute-start | bytes 322568 | tf_op jit(solution)/shard_map/ppermute | solution.py:25
  31.7 6.6 %collective-permute-done = f32[3,35,256]{2,1,0:T(8,128)S(1)} collective-permute-done((f32[3,35,256]{2,1,0:T(8,128)S(1)}, f32[3,35,256]{2,1,0:T(8,128)S(1)}, u32[]{:S(2)}, u32[]{:S(2)}) %collective-permute-start) | collective-permute-done | bytes 107552 | tf_op jit(solution)/shard_map/ppermute | solution.py:25
  38.3 2.8 %collective-permute-start.1 = (f32[16,3,256]{2,1,0:T(4,128)S(1)}, f32[16,3,256]{2,1,0:T(4,128)S(1)}, u32[]{:S(2)}, u32[]{:S(2)}) collective-permute-start(f32[16,3,256]{2,1,0:T(4,128)S(1)} %slice.129), channel_id=1, source_target_pairs={{7,0},{0,1},{1,2},{2,3},{3,4},{4,5},{5,6},{6,7},{15,8},{8,9},{9,10... | collective-permute-start | bytes 147464 | tf_op jit(solution)/shard_map/ppermute | solution.py:25
  41.1 1.1 negate_multiply_fusion.2
  42.7 1.0 convolution_bitcast_fusion.1
  43.7 1.8 copy.18
  45.5 3.8 %all-to-all-start = ((f32[1,2,256,512]{3,1,0,2:T(2,128)}), f32[1,2,256,512]{3,1,0,2:T(2,128)S(1)}, u32[]{:S(2)}, u32[]{:S(2)}) async-start(f32[1,2,256,512]{3,1,0,2:T(2,128)} %copy.18), calls=%async_computation | async-start | bytes 2097152 | tf_op jit(solution)/shard_map/all_to_all | solution.py:265
  49.4 1.1 fusion.43
  50.5 13.7 %all-to-all-done = f32[1,2,256,512]{3,1,0,2:T(2,128)S(1)} async-done(((f32[1,2,256,512]{3,1,0,2:T(2,128)}), f32[1,2,256,512]{3,1,0,2:T(2,128)S(1)}, u32[]{:S(2)}, u32[]{:S(2)}) %all-to-all-start) | async-done | bytes 1048608 | tf_op jit(solution)/shard_map/all_to_all | solution.py:265
  64.2 0.6 copy.29
  64.8 2.5 %reshape.304 = f32[16,2,16,16,32,1]{4,3,0,1,2,5:T(8,128)} reshape(f32[16,1,2,16,512]{4,0,2,3,1:T(8,128)S(1)} %bitcast.62) | data formatting | bytes 2097152 | tf_op jit(solution)/shard_map/reshape | solution.py:266
  67.3 9.1 %fusion.2 = f32[2,16,256,32]{2,3,0,1:T(8,128)S(1)} fusion(f32[16,2,16,16,32,1]{4,3,0,1,2,5:T(8,128)} %reshape.304, f32[1,1,256,16,16]{2,4,3,1,0:T(8,128)S(1)} %get-tuple-element.34, f32[1,1,256,16,16]{2,4,3,1,0:T(8,128)S(1)} %get-tuple-element.33, f32[1,1,256,16,16]{2,4,3,1,0:T(8,128)S(1)} %get-tuple-element.32), kind=kOutput, calls=%fused_computation.2 | convolution fusion | flops 1611399168 | bytes 2883584 | tf_op jit(solution)/shard_map/ocKst,scktz->okKz/dot_general | solution.py:268
  76.4 2.7 %copy.20 = f32[2,16,256,32]{3,2,1,0:T(8,128)} copy(f32[2,16,256,32]{2,3,0,1:T(8,128)S(1)} %fusion.2) | data formatting | bytes 2097152 | tf_op jit(solution)/shard_map/ocKst,scktz->okKz/transpose | solution.py:268
  79.1 3.7 %reshape_broadcast_in_dim_reshape.3 = f32[1,2,16,8,1024]{4,3,2,1,0:T(8,128)S(1)} reshape(f32[2,16,256,32]{3,2,1,0:T(8,128)} %copy.20) | data formatting | bytes 2097152 | tf_op jit(solution)/shard_map/reshape;broadcast_in_dim;reshape | solution.py:30
  82.8 0.6 reshape.301
  83.9 7.2 %all_to_all.25 = f32[4,2,1,2,16,1024]{5,0,3,4,2,1:T(4,128)S(1)} all-to-all(f32[4,2,1,2,16,1024]{5,0,3,4,2,1:T(4,128)S(1)} %copy.21), channel_id=1, replica_groups=mesh['gx_0'=4,'gx_1'=4,'gy_0'=4,'gy_1'=2] {'gy_1'}, dimensions={1} | all-to-all | bytes 2097152 | tf_op jit(solution)/shard_map/all_to_all | solution.py:44
  91.1 1.8 copy.22
  92.9 5.1 %all-to-all-start.2 = ((f32[4,2,1,2,16,1024]{5,1,3,4,2,0:T(2,128)}), f32[4,2,1,2,16,1024]{5,1,3,4,2,0:T(2,128)S(1)}, u32[]{:S(2)}, u32[]{:S(2)}) async-start(f32[4,2,1,2,16,1024]{5,1,3,4,2,0:T(2,128)} %copy.22), calls=%async_computation.2 | async-start | bytes 2097152 | tf_op jit(solution)/shard_map/all_to_all | solution.py:44
  98.0 1.1 fusion.42
  99.2 13.3 %all-to-all-done.2 = f32[4,2,1,2,16,1024]{5,1,3,4,2,0:T(2,128)S(1)} async-done(((f32[4,2,1,2,16,1024]{5,1,3,4,2,0:T(2,128)}), f32[4,2,1,2,16,1024]{5,1,3,4,2,0:T(2,128)S(1)}, u32[]{:S(2)}, u32[]{:S(2)}) %all-to-all-start.2) | async-done | bytes 1048608 | tf_op jit(solution)/shard_map/all_to_all | solution.py:44
  112.6 3.1 %reshape.307 = f32[8,2,16,32,32,1]{4,3,0,1,2,5:T(8,128)} reshape(f32[4,2,1,2,16,1024]{5,1,0,3,4,2:T(2,128)S(1)} %copy.23) | data formatting | bytes 2097152 | tf_op jit(solution)/shard_map/reshape;reshape;reshape | solution.py:272
  115.8 5.8 %convolution_bitcast_fusion.s_ref = f32[2,16,32,256]{3,2,1,0:T(8,128)S(1)} fusion(f32[8,2,16,32,32,1]{4,3,0,1,2,5:T(8,128)} %reshape.307, f32[1,1,256,8,32]{2,4,3,1,0:T(8,128)S(1)} %get-tuple-element.37, f32[1,1,256,8,32]{2,4,3,1,0:T(8,128)S(1)} %get-tuple-element.36, f32[1,1,256,8,32]{2,4,3,1,0:T(8,128)S(1)} %get-tuple-element.35), kind=kOutput, calls=%fused_computation.3 | convolution fusion | flops 1611399168 | bytes 2883584 | tf_op jit(solution)/shard_map/whzir,ihnqr->wnqz/dot_general | solution.py:274
  121.5 5.3 %epilogue.1 = (f32[2,16,32,256]{3,2,1,0:T(8,128)}, f32[8,256]{1,0:T(8,128)S(1)}) custom-call(f32[2,16,32,256]{3,2,1,0:T(8,128)S(1)} %convolution_bitcast_fusion.s_ref, f32[16,32,256]{2,1,0:T(8,128)S(1)} %copy-done.2, s32[16,32,256]{2,1,0:T(8,128)S(1)} %copy-done.3, s32[2]{0:T(128)S(1)} %pad_add_fusion.first_ref), custom_call_target="tpu_custom_call" | custom-call | tf_op jit(solution)/shard_map/epilogue/pallas_call | solution.py:232
  126.8 63.2 %psum.7 = f32[8,256]{1,0:T(8,128)S(1)} all-reduce(f32[8,256]{1,0:T(8,128)S(1)} %get-tuple-element.31), channel_id=1, replica_groups=mesh['gx_0'=4,'gx_1'=4,'gy_0'=4,'gy_1'=2] {'gx_0','gx_1','gy_0','gy_1'}, use_global_device_ids=true, to_apply=%region_0.0 | all-reduce | flops 2048 | bytes 16384 | tf_op jit(solution)/shard_map/psum | solution.py:279
  190.2 0.7 fusion.48
  191.0 0.6 slice_multiply_fusion
  191.5 1.4 stack.49
  193.0 1.2 subtract_multiply_fusion
  (28 shorter events, 1.7 us)
Async XLA Ops:
  0.6 1.0 copy-start
  1.7 1.0 copy-start.1
  2.7 0.9 copy-start.4
  29.4 8.8 %collective-permute-start = (f32[3,35,256]{2,1,0:T(8,128)S(1)}, f32[3,35,256]{2,1,0:T(8,128)S(1)}, u32[]{:S(2)}, u32[]{:S(2)}) collective-permute-start(f32[3,35,256]{2,1,0:T(8,128)S(1)} %pad_maximum_fusion), channel_id=1, source_target_pairs={{120,0},{0,8},{8,16},{16,24},{24,32},{32,40},{40,48},{48,56},{56,6... | collective-permute-start | bytes 322568 | tf_op jit(solution)/shard_map/ppermute | solution.py:25
  38.3 4.1 %collective-permute-start.1 = (f32[16,3,256]{2,1,0:T(4,128)S(1)}, f32[16,3,256]{2,1,0:T(4,128)S(1)}, u32[]{:S(2)}, u32[]{:S(2)}) collective-permute-start(f32[16,3,256]{2,1,0:T(4,128)S(1)} %slice.129), channel_id=1, source_target_pairs={{7,0},{0,1},{1,2},{2,3},{3,4},{4,5},{5,6},{6,7},{15,8},{8,9},{9,10... | collective-permute-start | bytes 147464 | tf_op jit(solution)/shard_map/ppermute | solution.py:25
  45.5 18.7 %all-to-all-start = ((f32[1,2,256,512]{3,1,0,2:T(2,128)}), f32[1,2,256,512]{3,1,0,2:T(2,128)S(1)}, u32[]{:S(2)}, u32[]{:S(2)}) async-start(f32[1,2,256,512]{3,1,0,2:T(2,128)} %copy.18), calls=%async_computation | async-start | bytes 2097152 | tf_op jit(solution)/shard_map/all_to_all | solution.py:265
  92.9 19.6 %all-to-all-start.2 = ((f32[4,2,1,2,16,1024]{5,1,3,4,2,0:T(2,128)}), f32[4,2,1,2,16,1024]{5,1,3,4,2,0:T(2,128)S(1)}, u32[]{:S(2)}, u32[]{:S(2)}) async-start(f32[4,2,1,2,16,1024]{5,1,3,4,2,0:T(2,128)} %copy.22), calls=%async_computation.2 | async-start | bytes 2097152 | tf_op jit(solution)/shard_map/all_to_all | solution.py:44
  115.7 5.8 %copy-start.2 = (f32[16,32,256]{2,1,0:T(8,128)S(1)}, f32[16,32,256]{2,1,0:T(8,128)}, u32[]{:S(2)}) copy-start(f32[16,32,256]{2,1,0:T(8,128)} %influence_ref.1) | copy-start | bytes 1572868
  115.7 5.8 %copy-start.3 = (s32[16,32,256]{2,1,0:T(8,128)S(1)}, s32[16,32,256]{2,1,0:T(8,128)}, u32[]{:S(2)}) copy-start(s32[16,32,256]{2,1,0:T(8,128)} %shells_ref.1) | copy-start | bytes 1572868

commit v2 on v1

v2 whole, which is shorter than its diff:
```python
import functools
import math

import jax
import jax.numpy as jnp
import numpy as np
from jax import lax
from jax.experimental import pallas as pl
from jax.experimental.pallas import tpu as pltpu
from jax.sharding import PartitionSpec as P

MESH = 256
SHELLS = 256
SCREEN = 4096
ROWS = 688
CHUNK = 1024
NX = 16
NY = 8
PARTS = 4
MESHID = pl.DeviceIdType.MESH


def spline(frac):
    cube = frac * frac * frac
    square = frac * frac
    rest = 1.0 - frac
    return (
        rest * rest * rest / 6.0,
        (3.0 * cube - 6.0 * square + 4.0) / 6.0,
        (-3.0 * cube + 3.0 * square + 3.0 * frac + 1.0) / 6.0,
        cube / 6.0,
    )


def periodic(cell, weights, rows, dim):
    row = lax.broadcasted_iota(jnp.int32, (rows, 128), 0)
    low = jnp.broadcast_to(cell[dim : dim + 1] & (rows - 1), (rows, 128))
    high = jnp.broadcast_to(cell[dim : dim + 1] // rows, (rows, 128))
    step = (row - low) & (rows - 1)
    table = jnp.zeros((rows, 128), jnp.float32)
    for t in range(4):
        table = jnp.where(step == t, jnp.broadcast_to(weights[t], (rows, 128)), table)
    block = high + jnp.where(row < low, 1, 0)
    return table, block


def build(cells_ref, frac_ref, charge_ref, begin, yz_buf, x_buf, XR=8):
    for tile in range(CHUNK // 128):
        at = pl.ds(pl.multiple_of(begin + tile * 128, 128), 128)
        lanes = pl.ds(tile * 128, 128)
        cell = cells_ref[:, at]
        weights = spline(frac_ref[:, at])
        charge = charge_ref[:, at]
        table, block = periodic(cell, [charge * w[0:1] for w in weights], 8, 0)
        block = block & 31
        for group in range(16):
            pair = [jnp.where(block == 2 * group + h, table, 0.0) for h in range(2)]
            x_buf[pl.ds(16 * group, 16), lanes] = jnp.concatenate(pair, 0).astype(jnp.bfloat16)
        table, block = periodic(cell & 15, [w[1:2] for w in weights], 8, 1)
        wy = [jnp.where(block == h, table, 0.0) for h in range(3)]
        table, block = periodic(cell & 31, [w[2:3] for w in weights], 8, 2)
        wz = [jnp.where(block == h, table, 0.0) for h in range(5)]
        rows = [jnp.broadcast_to(wy[y // 8][y % 8 : y % 8 + 1], (8, 128)) for y in range(19)]
        order = [(q, y) for q in range(4) for y in range(16)] + [(q, y) for q in range(4) for y in range(16, 19)]
        for k in range(38):
            pair = [rows[y] * wz[q] for q, y in order[2 * k : 2 * k + 2]]
            yz_buf[pl.ds(16 * k, 16), lanes] = jnp.concatenate(pair, 0).astype(jnp.bfloat16)
        tail = []
        for z in range(3):
            one = jnp.broadcast_to(wz[4][z : z + 1], (8, 128))
            tail += [one * wy[h] for h in range(3)]
        tail.append(jnp.zeros((8, 128), jnp.float32))
        for k in range(5):
            pair = jnp.concatenate(tail[2 * k : 2 * k + 2], 0)
            yz_buf[pl.ds(608 + 16 * k, 16), lanes] = pair.astype(jnp.bfloat16)


def product(yz_buf, x_buf):
    return lax.dot_general(
        yz_buf[...], x_buf[...], (((1,), (1,)), ((), ())), preferred_element_type=jnp.float32
    )


def spread_kernel(cells_ref, frac_ref, charge_ref, out_ref, yz0, x0, yz1, x1):
    count = charge_ref.shape[1]
    trips = count // (2 * CHUNK)
    out_ref[...] = jnp.zeros_like(out_ref)
    build(cells_ref, frac_ref, charge_ref, 0, yz0, x0)

    def body(m, carry):
        build(cells_ref, frac_ref, charge_ref, (2 * m + 1) * CHUNK, yz1, x1)
        out_ref[...] += product(yz0, x0)
        nxt = jnp.minimum((2 * m + 2) * CHUNK, count - CHUNK)
        build(cells_ref, frac_ref, charge_ref, nxt, yz0, x0)
        out_ref[...] += product(yz1, x1)
        return carry

    lax.fori_loop(0, trips, body, 0)


def spread(cells, fractions, charges):
    count = charges.shape[0]
    return pl.pallas_call(
        spread_kernel,
        out_shape=jax.ShapeDtypeStruct((ROWS, MESH), jnp.float32),
        in_specs=[pl.BlockSpec(memory_space=pltpu.VMEM)] * 3,
        out_specs=pl.BlockSpec(memory_space=pltpu.VMEM),
        scratch_shapes=[
            pltpu.VMEM((ROWS, CHUNK), jnp.bfloat16),
            pltpu.VMEM((MESH, CHUNK), jnp.bfloat16),
        ] * 2,
        compiler_params=pltpu.CompilerParams(vmem_limit_bytes=48 << 20),
        name="spread",
    )(cells, fractions, charges.reshape(1, count))


def signed(index):
    return jnp.where(index < MESH // 2, index, index - MESH).astype(jnp.float32)

def slab_outputs(real, imag, influence, shells, wave_x, wave_y, wave_z):
    squared = wave_x * wave_x + (wave_y * wave_y + wave_z * wave_z)
    origin = squared > 0.0
    weight = jnp.where(origin, influence, 0.0)
    power = real * real + imag * imag
    value = weight * power
    coef = value * 2.0 * (1.0 + squared * (1.0 / SCREEN)) / jnp.where(origin, squared, 1.0)
    return weight * real, weight * imag, power, value, coef

def onehot_dot(power, shells):
    total = None
    for r in range(4):
        p = power[8 * r : 8 * r + 8]
        s = shells[8 * r : 8 * r + 8]
        high = s >> 4
        low = s & 15
        left = jnp.concatenate([jnp.where(high == b, p, 0.0) for b in range(16)], 0).astype(jnp.bfloat16)
        right = jnp.concatenate([jnp.where(low == b, 1.0, 0.0) for b in range(16)], 0).astype(jnp.bfloat16)
        part = lax.dot_general(left, right, (((1,), (1,)), ((), ())), preferred_element_type=jnp.float32)
        total = part if total is None else total + part
    return total

def thirds(x):
    a = x.astype(jnp.bfloat16)
    rest = x - a.astype(jnp.float32)
    b = rest.astype(jnp.bfloat16)
    c = (rest - b.astype(jnp.float32)).astype(jnp.bfloat16)
    return a, b, c

def pack_stats(hist, en, m0, m1, m2, wave_y, wave_z):
    row = lax.broadcasted_iota(jnp.int32, (128, 128), 0)
    col = lax.broadcasted_iota(jnp.int32, (128, 128), 1)
    diag = jnp.where((row & 7) == (col & 7), hist, 0.0)
    by_high = jnp.sum(diag.reshape(16, 8, 128), axis=1)
    pick = (lax.broadcasted_iota(jnp.int32, (128, 256), 0) >> 3) == (lax.broadcasted_iota(jnp.int32, (128, 256), 1) & 15)
    pick = jnp.where(pick, 1.0, 0.0).astype(jnp.bfloat16)
    wide = sum(jnp.dot(t, pick, preferred_element_type=jnp.float32) for t in thirds(by_high))
    own = lax.broadcasted_iota(jnp.int32, (16, 256), 0) == (lax.broadcasted_iota(jnp.int32, (16, 256), 1) >> 4)
    spectrum = jnp.sum(jnp.where(own, wide, 0.0), axis=0, keepdims=True)
    terms = [en, m2, m1 * wave_y, m1 * wave_z, m0 * wave_y * wave_y, m0 * wave_y * wave_z, m0 * wave_z * wave_z]
    sub = lax.broadcasted_iota(jnp.int32, (8, 256), 0)
    out = jnp.where(sub == 0, jnp.broadcast_to(spectrum, (8, 256)), 0.0)
    for n, t in enumerate(terms):
        line = jnp.sum(t.reshape(4, 8, 256), axis=0)
        line = jnp.sum(line, axis=0, keepdims=True)
        out = jnp.where(sub == n + 1, jnp.broadcast_to(line, (8, 256)), out)
    return out


def split_table(table):
    table = np.asarray(table, np.float64)
    high = table.astype(np.float32).astype(jnp.bfloat16)
    low = (table - high.astype(np.float64)).astype(np.float32).astype(jnp.bfloat16)
    return np.stack([high, low])

def turn(phase, period):
    angle = 2.0 * np.pi * (phase % period) / period
    return np.cos(angle), np.sin(angle)

def complex_block(cosine, sine):
    return np.stack([np.stack([cosine, sine]), np.stack([-sine, cosine])])

def dft_tables():
    small = MESH // NX // PARTS
    k = np.arange(MESH)
    cosine, sine = turn(k[:, None] * k[None, :], MESH)
    along_x = np.stack([cosine, -sine]) / 16.0
    along_x = along_x.reshape(2, NX, PARTS, small, MESH).transpose(2, 1, 0, 3, 4).reshape(512, MESH)
    j = np.arange(16)
    block = complex_block(*turn(j[:, None] * j[None, :], 16))
    first = np.einsum("dcks,ij->dikscj", block, np.eye(small)) / 16.0
    first = first.reshape(2 * small * 16, 16 * 2 * small)
    cosine, sine = turn(j[:, None] * j[None, :], MESH)
    twiddle = np.stack([cosine, -sine])[:, None, :, :, None] * np.ones((1, small, 1, 1, 8))
    twiddle = twiddle.reshape(2, small * 16, 128).astype(np.float32)
    block = complex_block(*turn(j[:, None] * j[None, :], 16)).reshape(2, 2, NY, 2, 16)
    second = np.einsum("dcjky,zw->cyzjdkw", block, np.eye(8)).reshape(256, 256)
    z = np.arange(MESH).reshape(4, 2, 4, 8).transpose(0, 2, 1, 3)
    block = complex_block(*turn(z[..., None] * k, MESH)) / 16.0
    third = block.transpose(2, 3, 1, 4, 5, 0, 6).reshape(512, 512)
    return split_table(along_x), split_table(first), twiddle, split_table(second), split_table(third)

def halves(value):
    high = value.astype(jnp.bfloat16)
    return high, (value - high.astype(jnp.float32)).astype(jnp.bfloat16)

def dot(a, b):
    return jnp.dot(a, b, preferred_element_type=jnp.float32)

def dot_nt(a, b):
    return lax.dot_general(a, b, (((1,), (1,)), ((), ())), preferred_element_type=jnp.float32)

def add_halo(mesh, ext, from_y, from_z, from_corner):
    for q in range(4):
        at = pl.ds(128 * q, 24)
        if q:
            mesh[at] = ext[at] + from_y[pl.ds(24 * q, 24)]
            rest = pl.ds(128 * q + 24, 104)
            mesh[rest] = ext[rest]
    sub = lax.broadcasted_iota(jnp.int32, (8, MESH), 0)
    for y in range(16):
        at = pl.ds(8 * y, 8)
        value = ext[at]
        if y < 3:
            value = value + from_y[at]
        for z in range(3):
            line = from_z[pl.ds(24 * z + y, 1)]
            if y < 3:
                line = line + from_corner[pl.ds(8 * z + y, 1)]
            value = value + jnp.where(sub == z, jnp.broadcast_to(line, (8, MESH)), 0.0)
        mesh[at] = value

def along_x(table, mesh, send):
    high, low = halves(mesh[...])
    for half in range(2):
        at = pl.ds(256 * half, 256)
        out = dot_nt(table[0, at], high) + dot_nt(table[0, at], low) + dot_nt(table[1, at], high)
        send[pl.ds(2 * half, 2)] = out.reshape(2, NX, 8, 512)

def along_y(first, twiddle, second, block, send):
    high, low = halves(block[...].reshape(128, 512))
    out = dot(jnp.concatenate([first[0], first[0]], 1), jnp.concatenate([high, low], 0)) + dot(first[1], high)
    real, imag = out[:64], out[64:]
    tr, ti = twiddle[0], twiddle[1]
    rows = []
    for q in range(4):
        a = real[:, 128 * q : 128 * q + 128]
        b = imag[:, 128 * q : 128 * q + 128]
        rows.append(jnp.concatenate([a * tr - b * ti, a * ti + b * tr], 1))
    high, low = halves(jnp.concatenate(rows, 0))
    out = dot(high, second[0]) + dot(low, second[0]) + dot(high, second[1])
    group = lax.broadcasted_iota(jnp.int32, (64, 128), 1) >> 5
    for j in range(NY):
        total = None
        for q in range(4):
            piece = out[64 * q : 64 * q + 64, 128 * (j // 4) : 128 * (j // 4) + 128]
            shift = (32 * (q - j % 4)) % 128
            if shift:
                piece = pltpu.roll(piece, shift, 1)
            total = piece if total is None else jnp.where(group == q, piece, total)
        send[j] = total

def along_z(third, block):
    odd = ((lax.broadcasted_iota(jnp.int32, (64, 128), 1) >> 3) & 1) == 1
    top, bottom = [], []
    for m in range(4):
        a = block[2 * m]
        b = block[2 * m + 1]
        top.append(jnp.where(odd, pltpu.roll(b, 8, 1), a))
        bottom.append(jnp.where(odd, b, pltpu.roll(a, 120, 1)))
    value = jnp.concatenate([jnp.concatenate(top, 1), jnp.concatenate(bottom, 1)], 0)
    high, low = halves(value)
    return dot(high, third[0]) + dot(low, third[0]) + dot(high, third[1])

def torus(me, d):
    return lax.rem(me // 4 + d // 4, 4) * 4 + lax.rem(lax.rem(me, 4) + d % 4, 4)

def back(me, d):
    return torus(me, (4 - d // 4) % 4 * 4 + (4 - d % 4) % 4)

ORDER = (1, 4, 3, 12, 5, 15, 7, 13, 2, 8, 6, 9, 14, 11, 10)

def mega_kernel(
    ext, influence_hbm, shells_hbm, ax_hbm, first_hbm, twiddle_hbm, second_hbm, third_hbm,
    pot_ref, spectrum_ref, energy_ref, virial_ref,
    influence, shells, ax, first, twiddle, second, third,
    mesh, from_y, from_z, from_corner, send1, recv1, send2, recv2, hist, m0, m1, m2, en, stat, statz, statx,
    load_sem, halo_send, halo_recv, send_sem1, recv_sem1, send_sem2, recv_sem2, send_sem3, recv_sem3,
):
    me_x = lax.axis_index("gx")
    me_y = lax.axis_index("gy")
    right_x, left_x = lax.rem(me_x + 1, NX), lax.rem(me_x + NX - 1, NX)
    right_y, left_y = lax.rem(me_y + 1, NY), lax.rem(me_y + NY - 1, NY)

    loads = [
        pltpu.make_async_copy(a, b, load_sem.at[n])
        for n, (a, b) in enumerate(
            [(ax_hbm, ax), (first_hbm, first), (twiddle_hbm, twiddle), (second_hbm, second), (third_hbm, third),
             (influence_hbm, influence), (shells_hbm, shells)]
        )
    ]
    for load in loads:
        load.start()

    barrier = pltpu.get_barrier_semaphore()
    peers = [{"gx": torus(me_x, d), "gy": me_y} for d in range(1, NX)]
    peers += [{"gx": me_x, "gy": lax.rem(me_y + d, NY)} for d in range(1, NY)]
    peers += [{"gx": right_x, "gy": right_y}, {"gx": left_x, "gy": left_y}]
    for peer in peers:
        pl.semaphore_signal(barrier, inc=1, device_id=peer, device_id_type=MESHID)
    pl.semaphore_wait(barrier, len(peers))

    def remote(src, dst, send_sem, recv_sem, gx, gy):
        return pltpu.make_async_remote_copy(
            src_ref=src, dst_ref=dst, send_sem=send_sem, recv_sem=recv_sem,
            device_id={"gx": gx, "gy": gy}, device_id_type=MESHID,
        )

    halo = [
        remote(ext.at[pl.ds(512, 96)], from_y, halo_send.at[0], halo_recv.at[0], right_x, me_y),
        remote(ext.at[pl.ds(608, 72)], from_z, halo_send.at[1], halo_recv.at[1], me_x, right_y),
    ]
    for z in range(3):
        halo.append(remote(ext.at[pl.ds(608 + 24 * z + 16, 8)], from_corner.at[pl.ds(8 * z, 8)],
                           halo_send.at[2 + z], halo_recv.at[2 + z], right_x, right_y))
    for copy in halo:
        copy.start()
    for copy in halo:
        copy.wait()
    add_halo(mesh, ext, from_y, from_z, from_corner)
    loads[0].wait()
    along_x(ax, mesh, send1)
    exchange1 = []
    for part in range(PARTS):
        group = []
        for d in ORDER:
            to = torus(me_x, d)
            copy = remote(send1.at[part, to], recv1.at[part, me_x], send_sem1.at[part, d], recv_sem1.at[part, d], to, me_y)
            copy.start()
            group.append(copy)
        exchange1.append(group)
    for part in range(PARTS):
        recv1[part, me_x] = send1[part, me_x]
    for load in loads[1:]:
        load.wait()
    exchange2 = []
    for part in range(PARTS):
        for copy in exchange1[part]:
            copy.wait_recv()
        along_y(first, twiddle, second, recv1.at[part], send2.at[part])
        group = []
        for d in range(1, NY):
            to = lax.rem(me_y + d, NY)
            copy = remote(send2.at[part, to], recv2.at[part, me_y], send_sem2.at[part, d], recv_sem2.at[part, d], me_x, to)
            copy.start()
            group.append(copy)
        recv2[part, me_y] = send2[part, me_y]
        exchange2.append(group)

    first_x = me_x * 16
    wave_y = signed(me_y * 32 + lax.broadcasted_iota(jnp.int32, (32, MESH), 0))
    wave_z = signed(lax.broadcasted_iota(jnp.int32, (32, MESH), 1))
    for ref in (hist, m0, m1, m2, en):
        ref[...] = jnp.zeros_like(ref)
    for part in range(PARTS):
        for copy in exchange2[part]:
            copy.wait_recv()
        out = along_z(third, recv2.at[part])
        for n in range(4):
            k = 4 * part + n
            plane = jnp.concatenate([out[16 * n : 16 * n + 16], out[64 + 16 * n : 64 + 16 * n + 16]], 0)
            wave_x = signed(first_x + k)
            pr, pi, power, value, coef = slab_outputs(
                plane[:, :MESH], plane[:, MESH:], influence[k], shells[k], wave_x, wave_y, wave_z)
            pot_ref[0, k] = pr
            pot_ref[1, k] = pi
            hist[...] += onehot_dot(power, shells[k])
            en[...] += value
            m0[...] += coef
            m1[...] += coef * wave_x
            m2[...] += coef * (wave_x * wave_x)
    stat[...] = pack_stats(hist[...], en[...], m0[...], m1[...], m2[...], wave_y, wave_z)

    sums = []
    for d in range(1, NY):
        to = lax.rem(me_y + d, NY)
        sums.append(remote(stat, statz.at[me_y], send_sem3.at[0, d], recv_sem3.at[0, d], me_x, to))
        sums[-1].start()
    statz[me_y] = stat[...]
    for copy in sums:
        copy.wait()
    total = statz[0]
    for n in range(1, NY):
        total = total + statz[n]
    stat[...] = total
    sums = []
    for d in range(1, NX):
        to = torus(me_x, d)
        sums.append(remote(stat, statx.at[me_x], send_sem3.at[1, d], recv_sem3.at[1, d], to, me_y))
        sums[-1].start()
    statx[me_x] = stat[...]
    for copy in sums:
        copy.wait()
    total = statx[0]
    for n in range(1, NX):
        total = total + statx[n]
    spectrum_ref[...] = total[0:1] * (SHELLS / MESH**3)
    scale = 0.5 / MESH**3
    line = jnp.sum(total, axis=1, keepdims=True) * scale
    energy_ref[...] = line[1:2]
    row = lax.broadcasted_iota(jnp.int32, (3, 3), 0)
    col = lax.broadcasted_iota(jnp.int32, (3, 3), 1)
    pair = {(0, 0): 2, (0, 1): 3, (0, 2): 4, (1, 1): 5, (1, 2): 6, (2, 2): 7}
    virial = jnp.where(row == col, jnp.broadcast_to(line[1:2], (3, 3)), 0.0)
    for (a, b), n in pair.items():
        hit = ((row == a) & (col == b)) | ((row == b) & (col == a))
        virial = virial - jnp.where(hit, jnp.broadcast_to(line[n : n + 1], (3, 3)), 0.0)
    virial_ref[...] = virial
    for group in exchange1 + exchange2:
        for copy in group:
            copy.wait_send()


def mega(ext, influence, shells):
    tables = dft_tables()
    f32, bf16 = jnp.float32, jnp.bfloat16
    vmem = pl.BlockSpec(memory_space=pltpu.VMEM)
    anywhere = pl.BlockSpec(memory_space=pl.ANY)
    return pl.pallas_call(
        mega_kernel,
        out_shape=(
            jax.ShapeDtypeStruct((2,) + influence.shape, f32),
            jax.ShapeDtypeStruct((1, SHELLS), f32),
            jax.ShapeDtypeStruct((1, 1), f32),
            jax.ShapeDtypeStruct((3, 3), f32),
        ),
        in_specs=[vmem] + [anywhere] * 7,
        out_specs=(vmem,) * 4,
        scratch_shapes=[
            pltpu.VMEM(influence.shape, f32), pltpu.VMEM(shells.shape, jnp.int32),
            pltpu.VMEM((2, 512, MESH), bf16), pltpu.VMEM((2, 128, 128), bf16), pltpu.VMEM((2, 64, 128), f32),
            pltpu.VMEM((2, 256, 256), bf16), pltpu.VMEM((2, 512, 512), bf16),
            pltpu.VMEM((512, MESH), f32), pltpu.VMEM((96, MESH), f32), pltpu.VMEM((72, MESH), f32), pltpu.VMEM((24, MESH), f32),
            pltpu.VMEM((PARTS, NX, 8, 512), f32), pltpu.VMEM((PARTS, NX, 8, 512), f32),
            pltpu.VMEM((PARTS, NY, 64, 128), f32), pltpu.VMEM((PARTS, NY, 64, 128), f32),
            pltpu.VMEM((128, 128), f32)] + [pltpu.VMEM((32, MESH), f32)] * 4 + [
            pltpu.VMEM((8, MESH), f32), pltpu.VMEM((NY, 8, MESH), f32), pltpu.VMEM((NX, 8, MESH), f32),
            pltpu.SemaphoreType.DMA((7,)), pltpu.SemaphoreType.DMA((5,)), pltpu.SemaphoreType.DMA((5,)),
            pltpu.SemaphoreType.DMA((PARTS, NX)), pltpu.SemaphoreType.DMA((PARTS, NX)),
            pltpu.SemaphoreType.DMA((PARTS, NY)), pltpu.SemaphoreType.DMA((PARTS, NY)),
            pltpu.SemaphoreType.DMA((2, NX)), pltpu.SemaphoreType.DMA((2, NX)),
        ],
        compiler_params=pltpu.CompilerParams(collective_id=0, has_side_effects=True, vmem_limit_bytes=56 << 20),
        name="transform",
    )(ext, influence, shells, *tables)


def shards(cells, fractions, charges, influence, shells):
    extended = spread(cells, fractions, charges)
    potential_hat, spectrum, energy, virial = mega(extended, influence, shells)
    return potential_hat, energy.reshape(()), virial, spectrum.reshape(SHELLS)


def solution(mesh):
    both = ("gx", "gy")
    return jax.shard_map(
        shards,
        mesh=mesh,
        in_specs=(P(None, both), P(None, both), P(both), P("gx", "gy", None), P("gx", "gy", None)),
        out_specs=(P(None, "gx", "gy", None), P(), P(), P()),
        check_vma=False,
    )
```

time: 196 us -> 86.1 us (0.44)
  blocking collectives: 70.4 us -> 0 us
  Pallas kernels: 30.9 us -> 75.9 us
  waiting for transfers between devices: 33.8 us -> 0 us
  matrix products: 15.9 us -> 0 us
  local copies, waits for them, and re-layouts: 23 us -> 7.36 us
  starting transfers between devices: 13.9 us -> 0 us
  other arithmetic: 5.39 us -> 0 us
    psum x1 -> x0, blocking collectives: 63.2 us -> none  [shards(): stats = lax.psum(stats, GX_GY)]
    pallas_call x1, Pallas kernels: 5.25 us -> 49.9 us  [mega(): pl.pallas_call(mega_kernel, out_shape=(jax.ShapeDtypeStruct((2,) + influe...]
    all_to_all x2 -> x0, waiting for transfers between devices: 27 us -> none  [the longest x1 13.7 us: shards(): lax.all_to_all(along_x[None], GX, split_axis=2, concat_axis=0, tiled=True)]
    dot_general x3 -> x0, matrix products: 15.9 us -> none  [the longest x1 9.08 us: shards(): jnp.einsum('ocKst,scktz->okKz', table_y, moved, precision=upper_limit)]
    all_to_all x2 -> x0, starting transfers between devices: 8.95 us -> none  [the longest x1 5.11 us: moved_by_axis(): out = lax.all_to_all(out, axes[k], k, k, tiled=True)]
    another operation x3 -> x0, local copies, waits for them, and re-layouts: 8.23 us -> none  [the longest x1 3.74 us: cut_along(): shard.reshape(*lengths[:dim], peers, lengths[dim] // peers, *lengths[dim...]
    all_to_all x1 -> x0, blocking collectives: 7.21 us -> none  [moved_by_axis(): out = lax.all_to_all(out, axes[k], k, k, tiled=True)]
    ppermute x2 -> x0, waiting for transfers between devices: 6.79 us -> none  [passed_along(): return lax.ppermute(block, axis, route)]
  transfers between devices with their start and end apart: 4 -> 0, of which waited for: 4 -> 0; matrix products, arithmetic and copies ran while one was open for 2% -> 0% of each run, Pallas kernels for 0% -> 0%
where the time goes in v2:
time: 86.1 us; the launch traced here: 85.7 us
  Pallas kernels  75.9 us (88%)
  local copies, waits for them, and re-layouts  7.36 us (9%)
  between operations  2.44 us (3%)
    pallas_call x1, Pallas kernels, mega(): pl.pallas_call(mega_kernel, out_shape=(jax.ShapeDtypeStruct((2,) + influe...  49.9 us
    pallas_call x1, Pallas kernels, spread(): pl.pallas_call(spread_kernel, out_shape=jax.ShapeDtypeStruct((ROWS, MESH)...  26.1 us
    unnamed x15, local copies, waits for them, and re-layouts  7.36 us

profile of v2, /device:TPU:1, one launch (start us, length us, event | category | flops | bytes accessed | tf_op | source)
XLA Modules:
  0.0 85.7 jit_solution(14523227734522677009)
XLA Ops:
  0.6 0.0 copy-start.1
  0.6 1.0 %copy-done.1 = s32[3,32768]{1,0:T(4,128)S(1)} copy-done((s32[3,32768]{1,0:T(4,128)S(1)}, s32[3,32768]{1,0:T(4,128)}, u32[]{:S(2)}) %copy-start.1) | copy-done | bytes 393240
  1.7 0.0 copy-start.2
  1.7 1.0 %copy-done.2 = f32[3,32768]{1,0:T(4,128)S(1)} copy-done((f32[3,32768]{1,0:T(4,128)S(1)}, f32[3,32768]{1,0:T(4,128)}, u32[]{:S(2)}) %copy-start.2) | copy-done | bytes 393240
  2.7 0.0 copy-start.3
  2.7 0.9 %copy-done.3 = f32[32768]{0:T(1024)S(1)} copy-done((f32[32768]{0:T(1024)S(1)}, f32[32768]{0:T(1024)}, u32[]{:S(2)}) %copy-start.3) | copy-done | bytes 131096
  3.6 26.1 %spread.1.ext = f32[688,256]{1,0:T(8,128)S(1)} custom-call(s32[3,32768]{1,0:T(4,128)S(1)} %copy-done.1, f32[3,32768]{1,0:T(4,128)S(1)} %copy-done.2, f32[1,32768]{1,0:T(1,128)S(1)} %bitcast.3), custom_call_target="tpu_custom_call" | custom-call | tf_op jit(solution)/shard_map/spread/pallas_call | solution.py:103
  29.7 0.0 copy-start
  29.7 0.8 copy-done
  30.5 49.9 %transform.1 = (f32[2,16,32,256]{3,2,1,0:T(8,128)}, f32[1,256]{1,0:T(1,128)}, f32[1,1]{1,0:T(1,128)}, f32[3,3]{1,0:T(4,128)}) custom-call(f32[688,256]{1,0:T(8,128)} %copy-done, f32[16,32,256]{2,1,0:T(8,128)} %influence_hbm.1, s32[16,32,256]{2,1,0:T(8,128)} %shells_hbm.1, bf16[2,512,256]{2,1,0:T(8,128)(2,1)} %constant.10.clone.ax_hbm, ...), custom_call_target="tpu_custom_call" | custom-call | tf_op jit(solution)/shard_map/transform/pallas_call | solution.py:428
  80.4 0.0 copy-start.4
  80.4 2.3 %copy.18 = f32[2,16,32,256]{3,2,1,0:T(8,128)} copy(f32[2,16,32,256]{3,2,1,0:T(8,128)} %get-tuple-element.16) | data formatting | bytes 2097152
  83.4 0.0 copy-done.4
  83.4 0.0 copy-start.5
  83.4 0.6 copy.20
  84.0 0.1 copy-done.5
  84.0 0.6 copy.21
Async XLA Ops:
  0.6 1.0 %copy-start.1 = (s32[3,32768]{1,0:T(4,128)S(1)}, s32[3,32768]{1,0:T(4,128)}, u32[]{:S(2)}) copy-start(s32[3,32768]{1,0:T(4,128)} %cells_ref.1) | copy-start | bytes 1179652
  1.7 1.0 %copy-start.2 = (f32[3,32768]{1,0:T(4,128)S(1)}, f32[3,32768]{1,0:T(4,128)}, u32[]{:S(2)}) copy-start(f32[3,32768]{1,0:T(4,128)} %frac_ref.1) | copy-start | bytes 1179652
  2.7 0.9 %copy-start.3 = (f32[32768]{0:T(1024)S(1)}, f32[32768]{0:T(1024)}, u32[]{:S(2)}) copy-start(f32[32768]{0:T(1024)} %param.12) | copy-start | bytes 393220
  29.7 0.9 copy-start
  80.4 2.9 %copy-start.4 = (f32[3,3]{1,0:T(4,128)S(1)}, f32[3,3]{1,0:T(4,128)}, u32[]{:S(2)}) copy-start(f32[3,3]{1,0:T(4,128)} %get-tuple-element.18) | copy-start | bytes 112
  83.4 0.7 copy-start.5

commit v3 on v2

v3 whole, which is shorter than its diff:
```python
import functools
import math

import jax
import jax.numpy as jnp
import numpy as np
from jax import lax
from jax.experimental import pallas as pl
from jax.experimental.pallas import tpu as pltpu
from jax.sharding import PartitionSpec as P

MESH = 256
SHELLS = 256
SCREEN = 4096
ROWS = 688
CHUNK = 2048
NX = 16
NY = 8
PARTS = 4
SMALL = 16 // PARTS
VLIM = 44
MESHID = pl.DeviceIdType.MESH


def spline(frac):
    cube = frac * frac * frac
    square = frac * frac
    rest = 1.0 - frac
    return (
        rest * rest * rest * (1.0 / 6.0),
        (3.0 * cube - 6.0 * square + 4.0) * (1.0 / 6.0),
        (-3.0 * cube + 3.0 * square + 3.0 * frac + 1.0) * (1.0 / 6.0),
        cube * (1.0 / 6.0),
    )


def wide(line):
    return jnp.broadcast_to(line, (8, 128))


def periodic(low, high, weights, dim):
    row = lax.broadcasted_iota(jnp.int32, (8, 128), 0)
    ahead = row - wide(low[dim : dim + 1])
    step = ahead & 7
    table = jnp.where(step == 3, wide(weights[3]), 0.0)
    for t in range(3):
        table = jnp.where(step == t, wide(weights[t]), table)
    block = wide(high[dim : dim + 1]) + lax.shift_right_logical(ahead, 31)
    return table, block


def build(cells_ref, frac_ref, charge_ref, begin, yz_buf, x_buf):
    dims = lax.broadcasted_iota(jnp.int32, (3, 128), 0)
    inside = jnp.where(dims == 0, 255, jnp.where(dims == 1, 15, 31))
    for tile in range(CHUNK // 128):
        at = pl.ds(pl.multiple_of(begin + tile * 128, 128), 128)
        cell = cells_ref[:, at] & inside
        low = cell & 7
        high = lax.shift_right_logical(cell, 3)
        weights = spline(frac_ref[:, at])
        charge = charge_ref[:, at]
        table, block = periodic(low, high, [charge * w[0:1] for w in weights], 0)
        block = block & 31
        for group in range(32):
            x_buf[tile, pl.ds(8 * group, 8)] = jnp.where(block == group, table, 0.0)
        table, block = periodic(low, high, [w[1:2] for w in weights], 1)
        wy = [jnp.where(block == h, table, 0.0) for h in range(3)]
        table, block = periodic(low, high, [w[2:3] for w in weights], 2)
        wz = [jnp.where(block == h, table, 0.0) for h in range(5)]
        for y in range(19):
            one = wide(wy[y // 8][y % 8 : y % 8 + 1])
            for q in range(4):
                group = 16 * q + y if y < 16 else 64 + 3 * q + y - 16
                yz_buf[tile, pl.ds(8 * group, 8)] = one * wz[q]
        for z in range(3):
            one = wide(wz[4][z : z + 1])
            for h in range(3):
                yz_buf[tile, pl.ds(608 + 24 * z + 8 * h, 8)] = one * wy[h]


def product(yz_buf, x_buf):
    total = None
    for k in range(CHUNK // 256):
        rows = jnp.concatenate([yz_buf[2 * k], yz_buf[2 * k + 1]], 1)
        columns = jnp.concatenate([x_buf[2 * k], x_buf[2 * k + 1]], 1)
        part = lax.dot_general(rows, columns, (((1,), (1,)), ((), ())), preferred_element_type=jnp.float32)
        total = part if total is None else total + part
    return total


def atom_loads(cells_hbm, frac_hbm, charge_hbm, cells_ref, frac_ref, charge_ref, sems):
    count = charge_ref.shape[1]
    pieces = [pl.ds(0, CHUNK), pl.ds(CHUNK, count - CHUNK)]
    pairs = [(cells_hbm, cells_ref), (frac_hbm, frac_ref), (charge_hbm, charge_ref)]
    return [
        [pltpu.make_async_copy(a.at[:, piece], b.at[:, piece], sems.at[n, m]) for m, (a, b) in enumerate(pairs)]
        for n, piece in enumerate(pieces)
    ]


def spread_atoms(pieces, cells_ref, frac_ref, charge_ref, out_ref, yz0, x0, yz1, x1):
    count = charge_ref.shape[1]
    trips = count // (2 * CHUNK)

    out_ref[...] = jnp.zeros_like(out_ref)
    for yz in (yz0, yz1):
        yz[:, pl.ds(ROWS - 8, 8), :] = jnp.zeros((CHUNK // 128, 8, 128), jnp.float32)
    for load in pieces[0]:
        load.wait()
    build(cells_ref, frac_ref, charge_ref, 0, yz0, x0)
    for load in pieces[1]:
        load.wait()

    def body(m, carry):
        build(cells_ref, frac_ref, charge_ref, (2 * m + 1) * CHUNK, yz1, x1)
        out_ref[...] += product(yz0, x0)
        nxt = jnp.minimum((2 * m + 2) * CHUNK, count - CHUNK)
        build(cells_ref, frac_ref, charge_ref, nxt, yz0, x0)
        out_ref[...] += product(yz1, x1)
        return carry

    lax.fori_loop(0, trips - 1, body, 0)
    build(cells_ref, frac_ref, charge_ref, count - CHUNK, yz1, x1)
    out_ref[...] += product(yz0, x0)
    out_ref[...] += product(yz1, x1)


def signed(index):
    return jnp.where(index < MESH // 2, index, index - MESH).astype(jnp.float32)

def slab_outputs(real, imag, influence, shells, wave_x, wave_y, wave_z):
    squared = wave_x * wave_x + (wave_y * wave_y + wave_z * wave_z)
    origin = squared > 0.0
    weight = jnp.where(origin, influence, 0.0)
    power = real * real + imag * imag
    value = weight * power
    coef = value * 2.0 * (1.0 + squared * (1.0 / SCREEN)) / jnp.where(origin, squared, 1.0)
    return weight * real, weight * imag, power, value, coef

def onehot_dot(power, shells):
    total = None
    for r in range(4):
        p = power[8 * r : 8 * r + 8]
        s = shells[8 * r : 8 * r + 8]
        high = s >> 4
        low = s & 15
        left = jnp.concatenate([jnp.where(high == b, p, 0.0) for b in range(16)], 0).astype(jnp.bfloat16)
        right = jnp.concatenate([jnp.where(low == b, 1.0, 0.0) for b in range(16)], 0).astype(jnp.bfloat16)
        part = lax.dot_general(left, right, (((1,), (1,)), ((), ())), preferred_element_type=jnp.float32)
        total = part if total is None else total + part
    return total

def thirds(x):
    a = x.astype(jnp.bfloat16)
    rest = x - a.astype(jnp.float32)
    b = rest.astype(jnp.bfloat16)
    c = (rest - b.astype(jnp.float32)).astype(jnp.bfloat16)
    return a, b, c

def pack_stats(hist, en, m0, m1, m2, wave_y, wave_z):
    row = lax.broadcasted_iota(jnp.int32, (128, 128), 0)
    col = lax.broadcasted_iota(jnp.int32, (128, 128), 1)
    diag = jnp.where((row & 7) == (col & 7), hist, 0.0)
    by_high = jnp.sum(diag.reshape(16, 8, 128), axis=1)
    pick = (lax.broadcasted_iota(jnp.int32, (128, 256), 0) >> 3) == (lax.broadcasted_iota(jnp.int32, (128, 256), 1) & 15)
    pick = jnp.where(pick, 1.0, 0.0).astype(jnp.bfloat16)
    wide = sum(jnp.dot(t, pick, preferred_element_type=jnp.float32) for t in thirds(by_high))
    own = lax.broadcasted_iota(jnp.int32, (16, 256), 0) == (lax.broadcasted_iota(jnp.int32, (16, 256), 1) >> 4)
    spectrum = jnp.sum(jnp.where(own, wide, 0.0), axis=0, keepdims=True)
    terms = [en, m2, m1 * wave_y, m1 * wave_z, m0 * wave_y * wave_y, m0 * wave_y * wave_z, m0 * wave_z * wave_z]
    sub = lax.broadcasted_iota(jnp.int32, (8, 128), 0)
    lane = lax.broadcasted_iota(jnp.int32, (8, 128), 1)
    out = jnp.where(sub == 0, jnp.broadcast_to(spectrum[:, :128], (8, 128)), 0.0)
    out = jnp.where(sub == 1, jnp.broadcast_to(spectrum[:, 128:], (8, 128)), out)
    for n, t in enumerate(terms):
        line = jnp.sum(t.reshape(4, 8, MESH), axis=0)
        line = line[:, :128] + line[:, 128:]
        line = jnp.sum(jnp.sum(line, axis=0, keepdims=True), axis=1, keepdims=True)
        out = jnp.where((sub == 2) & (lane == n), jnp.broadcast_to(line, (8, 128)), out)
    return out


def split_table(table):
    table = np.asarray(table, np.float64)
    high = table.astype(np.float32).astype(jnp.bfloat16)
    low = (table - high.astype(np.float64)).astype(np.float32).astype(jnp.bfloat16)
    return np.stack([high, low])

def turn(phase, period):
    angle = 2.0 * np.pi * (phase % period) / period
    return np.cos(angle), np.sin(angle)

def complex_block(cosine, sine):
    return np.stack([np.stack([cosine, sine]), np.stack([-sine, cosine])])

def dft_tables():
    small = MESH // NX // PARTS
    k = np.arange(MESH)
    cosine, sine = turn(k[:, None] * k[None, :], MESH)
    along_x = np.stack([cosine, -sine]) / 16.0
    along_x = along_x.reshape(2, NX, PARTS, small, MESH).transpose(2, 1, 0, 3, 4).reshape(512, MESH)
    j = np.arange(16)
    block = complex_block(*turn(j[:, None] * j[None, :], 16))
    first = np.einsum("dcks,ij->dikscj", block, np.eye(small)) / 16.0
    first = first.reshape(2 * small * 16, 16 * 2 * small)
    cosine, sine = turn(j[:, None] * j[None, :], MESH)
    twiddle = np.stack([cosine, -sine])[:, None, :, :, None] * np.ones((1, small, 1, 1, 8))
    twiddle = twiddle.reshape(2, small * 16, 128).astype(np.float32)
    block = complex_block(*turn(j[:, None] * j[None, :], 16)).reshape(2, 2, NY, 2, 16)
    second = np.einsum("dcjky,zw->cyzjdkw", block, np.eye(8)).reshape(256, 256)
    z = np.arange(MESH).reshape(4, 2, 4, 8).transpose(0, 2, 1, 3)
    block = complex_block(*turn(z[..., None] * k, MESH)) / 16.0
    third = block.transpose(2, 3, 1, 4, 5, 0, 6).reshape(512, 512)
    return split_table(along_x), split_table(first), twiddle, split_table(second), split_table(third)

def halves(value):
    high = value.astype(jnp.bfloat16)
    return high, (value - high.astype(jnp.float32)).astype(jnp.bfloat16)

def dot(a, b):
    return jnp.dot(a, b, preferred_element_type=jnp.float32)

def dot_nt(a, b):
    return lax.dot_general(a, b, (((1,), (1,)), ((), ())), preferred_element_type=jnp.float32)

def add_halo(mesh, ext, from_y, from_z, from_corner):
    for q in range(4):
        at = pl.ds(128 * q, 24)
        if q:
            mesh[at] = ext[at] + from_y[pl.ds(24 * q, 24)]
            rest = pl.ds(128 * q + 24, 104)
            mesh[rest] = ext[rest]
    sub = lax.broadcasted_iota(jnp.int32, (8, MESH), 0)
    for y in range(16):
        at = pl.ds(8 * y, 8)
        value = ext[at]
        if y < 3:
            value = value + from_y[at]
        for z in range(3):
            line = from_z[pl.ds(24 * z + y, 1)]
            if y < 3:
                line = line + from_corner[pl.ds(8 * z + y, 1)]
            value = value + jnp.where(sub == z, jnp.broadcast_to(line, (8, MESH)), 0.0)
        mesh[at] = value

def along_x(table, mesh, send, ready):
    high, low = halves(mesh[...])
    for half in range(2):
        at = pl.ds(256 * half, 256)
        out = dot_nt(table[0, at], high) + dot_nt(table[0, at], low) + dot_nt(table[1, at], high)
        some = pl.ds(PARTS // 2 * half, PARTS // 2)
        send[some] = out.reshape(PARTS // 2, NX, 2 * SMALL, 512)
        ready(half)

def along_y(first, twiddle, second, block, send):
    high, low = halves(block[...].reshape(32 * SMALL, 512))
    out = dot(jnp.concatenate([first[0], first[0]], 1), jnp.concatenate([high, low], 0)) + dot(first[1], high)
    rows = 16 * SMALL
    real, imag = out[:rows], out[rows:]
    tr, ti = twiddle[0], twiddle[1]
    lines = []
    for q in range(4):
        a = real[:, 128 * q : 128 * q + 128]
        b = imag[:, 128 * q : 128 * q + 128]
        lines.append(jnp.concatenate([a * tr - b * ti, a * ti + b * tr], 1))
    high, low = halves(jnp.concatenate(lines, 0))
    out = dot(high, second[0]) + dot(low, second[0]) + dot(high, second[1])
    group = lax.broadcasted_iota(jnp.int32, (rows, 128), 1) >> 5
    for j in range(NY):
        total = None
        for q in range(4):
            piece = out[rows * q : rows * q + rows, 128 * (j // 4) : 128 * (j // 4) + 128]
            shift = (32 * (q - j % 4)) % 128
            if shift:
                piece = pltpu.roll(piece, shift, 1)
            total = piece if total is None else jnp.where(group == q, piece, total)
        send[j] = total

def along_z(third, block):
    odd = ((lax.broadcasted_iota(jnp.int32, (16 * SMALL, 128), 1) >> 3) & 1) == 1
    top, bottom = [], []
    for m in range(4):
        a = block[2 * m]
        b = block[2 * m + 1]
        top.append(jnp.where(odd, pltpu.roll(b, 8, 1), a))
        bottom.append(jnp.where(odd, b, pltpu.roll(a, 120, 1)))
    value = jnp.concatenate([jnp.concatenate(top, 1), jnp.concatenate(bottom, 1)], 0)
    high, low = halves(value)
    return dot(high, third[0]) + dot(low, third[0]) + dot(high, third[1])

def torus(me, d):
    return lax.rem(me // 4 + d // 4, 4) * 4 + lax.rem(lax.rem(me, 4) + d % 4, 4)

def back(me, d):
    return torus(me, (4 - d // 4) % 4 * 4 + (4 - d % 4) % 4)

ORDER = (10, 11, 14, 9, 6, 2, 8, 5, 15, 7, 13, 1, 4, 3, 12)
ORDER_Y = (4, 3, 5, 2, 6, 7, 1)
ORDER_SUM = (10, 11, 14, 9, 6, 2, 8, 5, 15, 7, 13, 1, 4, 3, 12)


def whole_kernel(
    cells_hbm, frac_hbm, charge_hbm, influence_hbm, shells_hbm, ax_hbm, first_hbm, twiddle_hbm, second_hbm, third_hbm,
    pot_ref, result_ref,
    cells_ref, frac_ref, charge_ref, yz0, x0, yz1, x1, ext,
    influence, shells, ax, first, twiddle, second, third,
    mesh, from_y, from_z, from_corner, send1, recv1, send2, recv2, hist, m0, m1, m2, en, stat, statz, statx,
    atom_sem, load_sem, halo_send, halo_recv, send_sem1, recv_sem1, send_sem2, recv_sem2, send_sem3, recv_sem3,
):
    me_x = lax.axis_index("gx")
    me_y = lax.axis_index("gy")
    right_x, left_x = lax.rem(me_x + 1, NX), lax.rem(me_x + NX - 1, NX)
    right_y, left_y = lax.rem(me_y + 1, NY), lax.rem(me_y + NY - 1, NY)

    pieces = atom_loads(cells_hbm, frac_hbm, charge_hbm, cells_ref, frac_ref, charge_ref, atom_sem)
    for piece in pieces:
        for load in piece:
            load.start()
    loads = [
        pltpu.make_async_copy(a, b, load_sem.at[n])
        for n, (a, b) in enumerate(
            [(ax_hbm, ax), (first_hbm, first), (twiddle_hbm, twiddle), (second_hbm, second), (third_hbm, third),
             (influence_hbm, influence), (shells_hbm, shells)]
        )
    ]
    for load in loads:
        load.start()

    barrier = pltpu.get_barrier_semaphore()
    peers = [{"gx": torus(me_x, d), "gy": me_y} for d in range(1, NX)]
    peers += [{"gx": me_x, "gy": lax.rem(me_y + d, NY)} for d in range(1, NY)]
    peers += [{"gx": right_x, "gy": right_y}, {"gx": left_x, "gy": left_y}]
    for peer in peers:
        pl.semaphore_signal(barrier, inc=1, device_id=peer, device_id_type=MESHID)
    spread_atoms(pieces, cells_ref, frac_ref, charge_ref, ext, yz0, x0, yz1, x1)
    pl.semaphore_wait(barrier, len(peers))

    def remote(src, dst, send_sem, recv_sem, gx, gy):
        return pltpu.make_async_remote_copy(
            src_ref=src, dst_ref=dst, send_sem=send_sem, recv_sem=recv_sem,
            device_id={"gx": gx, "gy": gy}, device_id_type=MESHID,
        )

    halo = [
        remote(ext.at[pl.ds(512, 96)], from_y, halo_send.at[0], halo_recv.at[0], right_x, me_y),
        remote(ext.at[pl.ds(608, 72)], from_z, halo_send.at[1], halo_recv.at[1], me_x, right_y),
    ]
    for z in range(3):
        halo.append(remote(ext.at[pl.ds(608 + 24 * z + 16, 8)], from_corner.at[pl.ds(8 * z, 8)],
                           halo_send.at[2 + z], halo_recv.at[2 + z], right_x, right_y))
    for copy in halo:
        copy.start()
    for copy in halo:
        copy.wait()
    add_halo(mesh, ext, from_y, from_z, from_corner)
    loads[0].wait()
    exchange1 = []

    def ready(half):
        for part in range(PARTS // 2 * half, PARTS // 2 * (half + 1)):
            group = []
            for d in ORDER:
                to = torus(me_x, d)
                group.append(remote(
                    send1.at[part, to], recv1.at[part, me_x], send_sem1.at[part, d], recv_sem1.at[part, d], to, me_y))
                group[-1].start()
            exchange1.append(group)

    along_x(ax, mesh, send1, ready)
    for part in range(PARTS):
        recv1[part, me_x] = send1[part, me_x]
    for load in loads[1:]:
        load.wait()
    exchange2 = []
    for part in range(PARTS):
        for copy in exchange1[part]:
            copy.wait_recv()
        along_y(first, twiddle, second, recv1.at[part], send2.at[part])
        group = []
        for d in ORDER_Y:
            to = lax.rem(me_y + d, NY)
            copy = remote(send2.at[part, to], recv2.at[part, me_y], send_sem2.at[part, d], recv_sem2.at[part, d], me_x, to)
            copy.start()
            group.append(copy)
        recv2[part, me_y] = send2[part, me_y]
        exchange2.append(group)

    first_x = me_x * 16
    wave_y = signed(me_y * 32 + lax.broadcasted_iota(jnp.int32, (32, MESH), 0))
    wave_z = signed(lax.broadcasted_iota(jnp.int32, (32, MESH), 1))
    for ref in (hist, m0, m1, m2, en):
        ref[...] = jnp.zeros_like(ref)
    for part in range(PARTS):
        for copy in exchange2[part]:
            copy.wait_recv()
        out = along_z(third, recv2.at[part])
        for n in range(SMALL):
            k = SMALL * part + n
            low = 16 * (SMALL + n)
            plane = jnp.concatenate([out[16 * n : 16 * n + 16], out[low : low + 16]], 0)
            wave_x = signed(first_x + k)
            pr, pi, power, value, coef = slab_outputs(
                plane[:, :MESH], plane[:, MESH:], influence[k], shells[k], wave_x, wave_y, wave_z)
            pot_ref[0, k] = pr
            pot_ref[1, k] = pi
            hist[...] += onehot_dot(power, shells[k])
            en[...] += value
            m0[...] += coef
            m1[...] += coef * wave_x
            m2[...] += coef * (wave_x * wave_x)
    stat[...] = pack_stats(hist[...], en[...], m0[...], m1[...], m2[...], wave_y, wave_z)

    sums = []
    for d in ORDER_Y:
        to = lax.rem(me_y + d, NY)
        sums.append(remote(stat, statz.at[me_y], send_sem3.at[0, d], recv_sem3.at[0, d], me_x, to))
        sums[-1].start()
    statz[me_y] = stat[...]
    for copy in sums:
        copy.wait()
    total = statz[0]
    for n in range(1, NY):
        total = total + statz[n]
    stat[...] = total
    sums = []
    for d in ORDER_SUM:
        to = torus(me_x, d)
        sums.append(remote(stat, statx.at[me_x], send_sem3.at[1, d], recv_sem3.at[1, d], to, me_y))
        sums[-1].start()
    statx[me_x] = stat[...]
    for copy in sums:
        copy.wait()
    total = statx[0]
    for n in range(1, NX):
        total = total + statx[n]
    result_ref[...] = total
    for group in exchange1 + exchange2:
        for copy in group:
            copy.wait_send()


def last_kernel(pot, result, pot_hbm, spectrum_ref, energy_ref, virial_ref, sem):
    slabs = [(c, pl.ds(4 * n, 4)) for c in range(2) for n in range(4)]
    writes = [pltpu.make_async_copy(pot.at[at], pot_hbm.at[at], sem.at[n]) for n, at in enumerate(slabs)]
    for write in writes:
        write.start()
    total = result[...]
    spectrum_ref[:, pl.ds(0, 128)] = total[0:1] * (SHELLS / MESH**3)
    spectrum_ref[:, pl.ds(128, 128)] = total[1:2] * (SHELLS / MESH**3)
    line = total[2:3] * (0.5 / MESH**3)
    energy_ref[...] = line[:, 0:1]
    row = lax.broadcasted_iota(jnp.int32, (3, 3), 0)
    col = lax.broadcasted_iota(jnp.int32, (3, 3), 1)
    pair = {(0, 0): 1, (0, 1): 2, (0, 2): 3, (1, 1): 4, (1, 2): 5, (2, 2): 6}
    virial = jnp.where(row == col, jnp.broadcast_to(line[:, 0:1], (3, 3)), 0.0)
    for (a, b), n in pair.items():
        hit = ((row == a) & (col == b)) | ((row == b) & (col == a))
        virial = virial - jnp.where(hit, jnp.broadcast_to(line[:, n : n + 1], (3, 3)), 0.0)
    virial_ref[...] = virial
    for write in writes:
        write.wait()


def shards(cells, fractions, charges, influence, shells):
    tables = dft_tables()
    count = charges.shape[0]
    f32, bf16 = jnp.float32, jnp.bfloat16
    vmem = pl.BlockSpec(memory_space=pltpu.VMEM)
    anywhere = pl.BlockSpec(memory_space=pl.ANY)
    dma = pltpu.SemaphoreType.DMA
    pot, result = pl.pallas_call(
        whole_kernel,
        out_shape=(jax.ShapeDtypeStruct((2,) + influence.shape, f32), jax.ShapeDtypeStruct((8, 128), f32)),
        in_specs=[anywhere] * 10,
        out_specs=(vmem, vmem),
        scratch_shapes=[
            pltpu.VMEM((3, count), jnp.int32), pltpu.VMEM((3, count), f32), pltpu.VMEM((1, count), f32),
        ] + [pltpu.VMEM((CHUNK // 128, ROWS, 128), f32), pltpu.VMEM((CHUNK // 128, MESH, 128), f32)] * 2 + [
            pltpu.VMEM((ROWS, MESH), f32),
            pltpu.VMEM(influence.shape, f32), pltpu.VMEM(shells.shape, jnp.int32),
            pltpu.VMEM((2, 512, MESH), bf16), pltpu.VMEM((2, 32 * SMALL, 32 * SMALL), bf16), pltpu.VMEM((2, 16 * SMALL, 128), f32),
            pltpu.VMEM((2, 256, 256), bf16), pltpu.VMEM((2, 512, 512), bf16),
            pltpu.VMEM((512, MESH), f32), pltpu.VMEM((96, MESH), f32), pltpu.VMEM((72, MESH), f32), pltpu.VMEM((24, MESH), f32),
            pltpu.VMEM((PARTS, NX, 2 * SMALL, 512), f32), pltpu.VMEM((PARTS, NX, 2 * SMALL, 512), f32),
            pltpu.VMEM((PARTS, NY, 16 * SMALL, 128), f32), pltpu.VMEM((PARTS, NY, 16 * SMALL, 128), f32),
            pltpu.VMEM((128, 128), f32)] + [pltpu.VMEM((32, MESH), f32)] * 4 + [
            pltpu.VMEM((8, 128), f32), pltpu.VMEM((NY, 8, 128), f32), pltpu.VMEM((NX, 8, 128), f32),
            dma((2, 3)), dma((7,)), dma((5,)), dma((5,)),
            dma((PARTS, NX)), dma((PARTS, NX)), dma((PARTS, NY)), dma((PARTS, NY)), dma((2, NX)), dma((2, NX)),
        ],
        compiler_params=pltpu.CompilerParams(collective_id=0, has_side_effects=True, vmem_limit_bytes=VLIM << 20),
        name="whole",
    )(*[pltpu.with_memory_space_constraint(a, pltpu.HBM) for a in (cells, fractions, charges.reshape(1, count), influence, shells, *tables)])
    potential_hat, spectrum, energy, virial = pl.pallas_call(
        last_kernel,
        out_shape=(
            jax.ShapeDtypeStruct(pot.shape, f32),
            jax.ShapeDtypeStruct((1, SHELLS), f32),
            jax.ShapeDtypeStruct((1, 1), f32),
            jax.ShapeDtypeStruct((3, 3), f32),
        ),
        in_specs=[vmem] * 2,
        out_specs=(anywhere, vmem, vmem, vmem),
        scratch_shapes=[dma((8,))],
        compiler_params=pltpu.CompilerParams(vmem_limit_bytes=8 << 20),
        name="last",
    )(pot, result)
    return potential_hat, energy.reshape(()), virial, spectrum.reshape(SHELLS)


def solution(mesh):
    both = ("gx", "gy")
    return jax.shard_map(
        shards,
        mesh=mesh,
        in_specs=(P(None, both), P(None, both), P(both), P("gx", "gy", None), P("gx", "gy", None)),
        out_specs=(P(None, "gx", "gy", None), P(), P(), P()),
        check_vma=False,
    )
```

time: 86.1 us -> 63.6 us (0.74)
  Pallas kernels: 75.9 us -> 62.9 us
  local copies, waits for them, and re-layouts: 7.36 us -> 0 us
  between operations: 2.44 us -> 0.64 us
    pallas_call x2, Pallas kernels: 75.9 us -> 62.9 us  [the longest x1 61.2 us: shards(): pl.pallas_call(whole_kernel, out_shape=(jax.ShapeDtypeStruct((2,) + influ...]
    unnamed x15 -> x0, local copies, waits for them, and re-layouts: 7.36 us -> none
where the time goes in v3:
time: 63.6 us; the launch traced here: 63.5 us
  Pallas kernels  62.9 us (99%)
  between operations  0.64 us (1%)
    pallas_call x1, Pallas kernels, shards(): pl.pallas_call(whole_kernel, out_shape=(jax.ShapeDtypeStruct((2,) + influ...  61.2 us
    pallas_call x1, Pallas kernels, shards(): pl.pallas_call(last_kernel, out_shape=(jax.ShapeDtypeStruct(pot.shape, f3...  1.61 us

profile of v3, /device:TPU:1, one launch (start us, length us, event | category | flops | bytes accessed | tf_op | source)
XLA Modules:
  0.0 63.5 jit_solution(5044651954313950193)
XLA Ops:
  0.6 61.2 %whole.1 = (f32[2,16,32,256]{3,2,1,0:T(8,128)S(1)}, f32[8,128]{1,0:T(8,128)S(1)}) custom-call(s32[3,32768]{1,0:T(4,128)} %cells_hbm.1, f32[3,32768]{1,0:T(4,128)} %frac_hbm.1, f32[1,32768]{1,0:T(1,128)} %bitcast.3, f32[16,32,256]{2,1,0:T(8,128)} %influence_hbm.1, s32[16,32,256]{2,1,0:T(8,128)} %shells_hbm.1, bf16[2,512,256]{2,1,0:T(8,128)(2,1)} %constant.10.clone.ax_hbm, ...), custom_call_target="tpu_custom_call" | custom-call | tf_op jit(solution)/shard_map/whole/pallas_call | solution.py:471
  61.9 1.6 %last.1 = (f32[2,16,32,256]{3,2,1,0:T(8,128)}, f32[1,256]{1,0:T(1,128)}, f32[1,1]{1,0:T(1,128)}, f32[3,3]{1,0:T(4,128)}) custom-call(f32[2,16,32,256]{3,2,1,0:T(8,128)S(1)} %get-tuple-element.10.pot, f32[8,128]{1,0:T(8,128)S(1)} %get-tuple-element.11.result), custom_call_target="tpu_custom_call" | custom-call | tf_op jit(solution)/shard_map/last/pallas_call | solution.py:494
